TPU v7x, 256 devices: a 2x2x32 block of a 4x8x32 slice. The times are simulated.
256 devices in a mesh: scan: 4 (over x, y), row: 64 (over z, core).
Axes of the slice: x: 2, y: 2, z: 32, core: 2. Of those that a mesh axis runs over, the one named last changes fastest.
The devices are a block of a 4x8x32 slice.
Arguments:
- object_field: float32 [2, 2, 32768, 768], P(None, None, ('scan', 'row')), parts along dimension 2, may hold values from -1 to 1
- row_offset: int32 [256], P(('scan', 'row')), parts along dimension 0, may hold values from 0 to 127
- col_offset: int32 [256], P(('scan', 'row')), parts along dimension 0, may hold values from 0 to 256
- amplitudes: float32 [256, 512, 512], P(('scan', 'row')), parts along dimension 0, may hold values from 0.2 to 2
- probe: float32 [8, 512, 512], P('scan'), parts along dimension 0, may hold values from -6 to 6
- phase: float32 [512, 512], replicated, may hold values from -3.140625 to 3.140625
Outputs:
- updated_object: float32 [2, 2, 32768, 768], P(None, None, ('scan', 'row')), parts along dimension 2
There are 4 independent parts, one for each index of `scan`. A program takes and returns all parts, laid end to end along the dimension named above; an argument that names none is the same for every part. Nothing has to cross between parts.
All inputs are finite; a program needn't handle non-finite values.
Results may differ from a plain program's by a relative error of at most 0.014.
Values sent between devices are 32-bit elements; how exact they have to be, the bound alone decides.
No kernel may reach another device: no remote copies, remote signals or barrier semaphores. Data moves between devices by JAX's collectives and lax.ppermute only.
A program may use at most 64 MiB of HBM per device.

v0:
```python
import math

import jax
import jax.numpy as jnp
from jax import lax
from jax.sharding import PartitionSpec as P


def shifted(block, axis, distance):
    devices = range(lax.axis_size(axis))
    route = [((i - distance) % len(devices), i) for i in devices]
    return lax.ppermute(block, axis, route)


def dft_mats(length, flip):
    index = jnp.arange(length, dtype=jnp.int32)
    angles = (index[:, None] * index[None, :] % length).astype(jnp.float32) * (
        -2.0 * math.pi / length
    )
    factor = 1.0 / math.sqrt(length)
    cos_table = (jnp.cos(angles) * factor).astype(jnp.bfloat16)
    sin_table = (jnp.sin(angles) * factor).astype(jnp.bfloat16)
    if flip:
        sin_table = -sin_table
    left_real = jnp.concatenate([cos_table, -sin_table], axis=1)
    left_imag = jnp.concatenate([sin_table, cos_table], axis=1)
    right_real = jnp.concatenate([cos_table, -sin_table], axis=0)
    right_imag = jnp.concatenate([sin_table, cos_table], axis=0)
    return (left_real, left_imag, right_real, right_imag)


def transform(real_part, imag_part, mats):
    left_real, left_imag, right_real, right_imag = mats
    stacked = jnp.concatenate(
        [real_part.astype(jnp.bfloat16), imag_part.astype(jnp.bfloat16)], axis=0
    )
    half_real = jnp.dot(left_real, stacked, preferred_element_type=jnp.float32).astype(jnp.bfloat16)
    half_imag = jnp.dot(left_imag, stacked, preferred_element_type=jnp.float32).astype(jnp.bfloat16)
    joined = jnp.concatenate([half_real, half_imag], axis=1)
    return (
        jnp.dot(joined, right_real, preferred_element_type=jnp.float32),
        jnp.dot(joined, right_imag, preferred_element_type=jnp.float32),
    )


def cmul(a_real, a_imag, b_real, b_imag):
    return (a_real * b_real - a_imag * b_imag, a_real * b_imag + a_imag * b_real)


def cmul_conj(a_real, a_imag, b_real, b_imag):
    return (a_real * b_real + a_imag * b_imag, a_real * b_imag - a_imag * b_real)


def window_gradient(window, probe, amplitude, phase, forward, inverse):
    prop_real = jnp.cos(phase)
    prop_imag = jnp.sin(phase)
    probe_real, probe_imag = (probe[0], probe[1])
    first_real, first_imag = (window[0, 0], window[0, 1])
    second_real, second_imag = (window[1, 0], window[1, 1])
    exit_real, exit_imag = cmul(probe_real, probe_imag, first_real, first_imag)
    freq_real, freq_imag = transform(exit_real, exit_imag, forward)
    moved_real, moved_imag = cmul(freq_real, freq_imag, prop_real, prop_imag)
    inner_real, inner_imag = transform(moved_real, moved_imag, inverse)
    wave_real, wave_imag = cmul(inner_real, inner_imag, second_real, second_imag)
    far_real, far_imag = transform(wave_real, wave_imag, forward)
    modulus = jnp.sqrt(far_real * far_real + far_imag * far_imag)
    ratio = amplitude / jnp.maximum(modulus, 0.1)
    resid_real = far_real * (1.0 - ratio)
    resid_imag = far_imag * (1.0 - ratio)
    back_real, back_imag = transform(resid_real, resid_imag, inverse)
    grad2_real, grad2_imag = cmul_conj(inner_real, inner_imag, back_real, back_imag)
    mid_real, mid_imag = cmul_conj(second_real, second_imag, back_real, back_imag)
    spec_real, spec_imag = transform(mid_real, mid_imag, forward)
    unprop_real, unprop_imag = cmul_conj(prop_real, prop_imag, spec_real, spec_imag)
    entry_real, entry_imag = transform(unprop_real, unprop_imag, inverse)
    grad1_real, grad1_imag = cmul_conj(probe_real, probe_imag, entry_real, entry_imag)
    return jnp.stack([jnp.stack([grad1_real, grad1_imag]), jnp.stack([grad2_real, grad2_imag])])


def body(object_field, row_offset, col_offset, amplitudes, probe, phase):
    strip_rows = object_field.shape[2]
    window_edge = probe.shape[1]
    anchor = jnp.int32(0)
    forward = dft_mats(window_edge, False)
    inverse = dft_mats(window_edge, True)
    pieces = {0: object_field}
    carried = object_field
    for owner in (1, 2, 3):
        carried = shifted(carried, "row", -1)
        pieces[owner] = carried
    carried = object_field
    for owner in (1, 2):
        carried = shifted(carried, "row", 1)
        pieces[-owner] = carried
    gathered = jnp.concatenate([pieces[owner] for owner in (-2, -1, 0, 1, 2, 3)], axis=2)
    row_start = strip_rows // 2 + row_offset[0]
    col_start = col_offset[0]
    window = lax.dynamic_slice(
        gathered, (anchor, anchor, row_start, col_start), (2, 2, window_edge, window_edge)
    )
    grads = window_gradient(window, probe, amplitudes[0], phase, forward, inverse)
    canvas = jnp.zeros(gathered.shape, jnp.float32)
    canvas = lax.dynamic_update_slice(canvas, grads, (anchor, anchor, row_start, col_start))
    blocks = [canvas[:, :, slot * strip_rows : (slot + 1) * strip_rows] for slot in range(6)]
    upward = jnp.zeros_like(blocks[0])
    for slot in (5, 4, 3):
        upward = shifted(upward + blocks[slot], "row", 1)
    downward = jnp.zeros_like(blocks[0])
    for slot in (0, 1):
        downward = shifted(downward + blocks[slot], "row", -1)
    total = blocks[2] + upward + downward
    return object_field - 0.5 * total


def solution(mesh):
    placed = (
        P(None, None, ("scan", "row"), None),
        P(("scan", "row")),
        P(("scan", "row")),
        P(("scan", "row"), None, None),
        P("scan", None, None),
        P(),
    )
    return jax.shard_map(
        body,
        mesh=mesh,
        in_specs=placed,
        out_specs=P(None, None, ("scan", "row"), None),
        check_vma=False,
    )
```

profile of v0, /device:TPU:38, one launch (start us, length us, event | category | flops | bytes accessed | tf_op | source)
XLA Modules:
  0.0 212.6 jit_solution(5776531752978583994)
XLA Ops:
  0.0 22.5 %collective-permute-start.2 = (f32[2,2,128,768]{3,2,1,0:T(8,128)}, f32[2,2,128,768]{3,2,1,0:T(8,128)S(1)}, u32[]{:S(2)}, u32[]{:S(2)}) collective-permute-start(f32[2,2,128,768]{3,2,1,0:T(8,128)} %param.6), channel_id=1, source_target_pairs={{1,0},{2,1},{3,2},{4,3},{5,4},{6,5},{7,6},{8,7},{9,8},{10,9},{11,1... | collective-permute-start | bytes 4718600 | tf_op jit(solution)/shard_map/ppermute | solution.py:12
  22.5 18.2 %collective-permute-done.2 = f32[2,2,128,768]{3,2,1,0:T(8,128)S(1)} collective-permute-done((f32[2,2,128,768]{3,2,1,0:T(8,128)}, f32[2,2,128,768]{3,2,1,0:T(8,128)S(1)}, u32[]{:S(2)}, u32[]{:S(2)}) %collective-permute-start.2) | collective-permute-done | bytes 1572896 | tf_op jit(solution)/shard_map/ppermute | solution.py:12
  40.8 3.0 %collective-permute-start.3 = (f32[2,2,128,768]{3,2,1,0:T(8,128)S(1)}, f32[2,2,128,768]{3,2,1,0:T(8,128)}, u32[]{:S(2)}, u32[]{:S(2)}) collective-permute-start(f32[2,2,128,768]{3,2,1,0:T(8,128)S(1)} %collective-permute-done.2), channel_id=1, source_target_pairs={{1,0},{2,1},{3,2},{4,3},{5,4},{6,5},{7,6},{8,7},{9,8},{10,9},{11,1... | collective-permute-start | bytes 4718600 | tf_op jit(solution)/shard_map/ppermute | solution.py:12
  43.8 17.9 %collective-permute-done.3 = f32[2,2,128,768]{3,2,1,0:T(8,128)} collective-permute-done((f32[2,2,128,768]{3,2,1,0:T(8,128)S(1)}, f32[2,2,128,768]{3,2,1,0:T(8,128)}, u32[]{:S(2)}, u32[]{:S(2)}) %collective-permute-start.3) | collective-permute-done | bytes 1572896 | tf_op jit(solution)/shard_map/ppermute | solution.py:12
  61.7 3.2 %collective-permute-start.4 = (f32[2,2,128,768]{3,2,1,0:T(8,128)}, f32[2,2,128,768]{3,2,1,0:T(8,128)}, u32[]{:S(2)}, u32[]{:S(2)}) collective-permute-start(f32[2,2,128,768]{3,2,1,0:T(8,128)} %collective-permute-done.3), channel_id=1, source_target_pairs={{1,0},{2,1},{3,2},{4,3},{5,4},{6,5},{7,6},{8,7},{9,8},{10,9},{11,1... | collective-permute-start | bytes 4718600 | tf_op jit(solution)/shard_map/ppermute | solution.py:12
  66.3 4.0 %fusion.30 = bf16[512,512]{1,0:T(8,128)(2,1)S(1)} fusion(), kind=kLoop, calls=%fused_computation.99 | loop fusion | flops 4980736 | bytes 524288 | tf_op jit(solution)/shard_map/neg | solution.py:24
  70.3 4.4 %multiply_convert_fusion.2 = (bf16[512,512]{1,0:T(8,128)(2,1)S(1)}, bf16[512,512]{1,0:T(8,128)(2,1)S(1)}) fusion(), kind=kLoop, calls=%fused_computation.82 | loop fusion | flops 4718592 | bytes 1048576 | tf_op jit(solution)/shard_map/convert_element_type | solution.py:22
  74.7 3.9 %fusion.55 = (f32[512,512]{1,0:T(8,128)S(1)}, f32[512,512]{1,0:T(8,128)S(1)}) fusion(f32[512,512]{1,0:T(8,128)S(1)} %copy-done.5), kind=kLoop, calls=%fused_computation.130 | loop fusion | bytes 3145728 | tf_op jit(solution)/shard_map/sin | solution.py:56
  78.6 1.6 constant_dynamic-update-slice_fusion.5
  80.6 1.3 copy-done.1
  82.1 1.5 constant_dynamic-update-slice_fusion.1
  83.7 1.7 constant_dynamic-update-slice_fusion
  88.7 0.9 subtract_convert_fusion.3
  89.6 0.8 convolution_convert_fusion.9
  91.9 1.1 subtract_convert_fusion.2
  95.7 1.2 multiply_convert_fusion.1
  97.6 0.8 convolution_convert_fusion.4
  99.9 1.2 add_convert_fusion.1
  103.3 0.8 add_convert_fusion
  104.2 0.8 convolution_convert_fusion.1
  106.4 0.8 fusion.12
  107.6 2.5 %pad_maximum_fusion = f32[2,2,512,512]{3,2,1,0:T(8,128)} fusion(f32[1,2,512,512]{3,2,1,0:T(8,128)S(1)} %maximum_bitcast_fusion.1, f32[1,2,512,512]{3,2,1,0:T(8,128)S(1)} %maximum_bitcast_fusion), kind=kLoop, calls=%fused_computation | loop fusion | flops 1048576 | bytes 8388608 | tf_op jit(solution)/shard_map/stack | solution.py:77
  110.2 4.5 %broadcast_in_dim.2 = f32[2,2,768,768]{3,2,1,0:T(8,128)} broadcast(f32[]{:T(128)} %constant.27.clone.1), dimensions={} | broadcast | bytes 9437188 | tf_op jit(solution)/shard_map/broadcast_in_dim | solution.py:102
  114.6 28.8 %dynamic_update_slice.3 = f32[2,2,768,768]{3,2,1,0:T(8,128)} dynamic-update-slice(f32[2,2,768,768]{3,2,1,0:T(8,128)} %broadcast_in_dim.2, f32[2,2,512,512]{3,2,1,0:T(8,128)} %pad_maximum_fusion, s32[]{:T(128)} %constant.28.clone.1, s32[]{:T(128)} %constant.28.clone.1, s32[]{:T(128)S(6)} %select_n.48, s32[]{:T(128)S(6)} %select_n.49) | dynamic-update-slice | bytes 8388612 | tf_op jit(solution)/shard_map/dynamic_update_slice | solution.py:103
  143.4 1.7 slice.49
  145.2 21.0 %collective-permute-done.5 = f32[2,2,128,768]{3,2,1,0:T(8,128)S(1)} collective-permute-done((f32[2,2,128,768]{3,2,1,0:T(8,128)S(1)}, f32[2,2,128,768]{3,2,1,0:T(8,128)S(1)}, u32[]{:S(2)}, u32[]{:S(2)}) %collective-permute-start.5) | collective-permute-done | bytes 1572896 | tf_op jit(solution)/shard_map/ppermute | solution.py:12
  166.2 2.2 %slice_add_fusion.2 = (f32[2,2,128,768]{3,2,1,0:T(8,128)S(1)}, f32[2,2,128,768]{3,2,1,0:T(8,128)S(1)}) fusion(f32[2,2,128,768]{3,2,1,0:T(8,128)S(1)} %collective-permute-done.5, f32[2,2,768,768]{3,2,1,0:T(8,128)} %dynamic_update_slice.3), kind=kLoop, calls=%fused_computation.5 | loop fusion | flops 393216 | bytes 7864320 | tf_op jit(solution)/shard_map/add | solution.py:107
  168.5 2.9 %collective-permute-start.8 = (f32[2,2,128,768]{3,2,1,0:T(8,128)S(1)}, f32[2,2,128,768]{3,2,1,0:T(8,128)S(1)}, u32[]{:S(2)}, u32[]{:S(2)}) collective-permute-start(f32[2,2,128,768]{3,2,1,0:T(8,128)S(1)} %get-tuple-element.14), channel_id=1, source_target_pairs={{1,0},{2,1},{3,2},{4,3},{5,4},{6,5},{7,6},{8,7},{9,8},{10,9},{11,1... | collective-permute-start | bytes 4718600 | tf_op jit(solution)/shard_map/ppermute | solution.py:12
  171.4 18.1 %collective-permute-done.6 = f32[2,2,128,768]{3,2,1,0:T(8,128)S(1)} collective-permute-done((f32[2,2,128,768]{3,2,1,0:T(8,128)S(1)}, f32[2,2,128,768]{3,2,1,0:T(8,128)S(1)}, u32[]{:S(2)}, u32[]{:S(2)}) %collective-permute-start.6) | collective-permute-done | bytes 1572896 | tf_op jit(solution)/shard_map/ppermute | solution.py:12
  190.0 3.0 %collective-permute-start.9 = (f32[2,2,128,768]{3,2,1,0:T(8,128)S(1)}, f32[2,2,128,768]{3,2,1,0:T(8,128)S(1)}, u32[]{:S(2)}, u32[]{:S(2)}) collective-permute-start(f32[2,2,128,768]{3,2,1,0:T(8,128)S(1)} %get-tuple-element.12), channel_id=1, source_target_pairs={{1,0},{2,1},{3,2},{4,3},{5,4},{6,5},{7,6},{8,7},{9,8},{10,9},{11,1... | collective-permute-start | bytes 4718600 | tf_op jit(solution)/shard_map/ppermute | solution.py:12
  193.0 18.0 %collective-permute-done.7 = f32[2,2,128,768]{3,2,1,0:T(8,128)S(1)} collective-permute-done((f32[2,2,128,768]{3,2,1,0:T(8,128)S(1)}, f32[2,2,128,768]{3,2,1,0:T(8,128)S(1)}, u32[]{:S(2)}, u32[]{:S(2)}) %collective-permute-start.7) | collective-permute-done | bytes 1572896 | tf_op jit(solution)/shard_map/ppermute | solution.py:12
  211.0 1.5 fusion.2
  (46 shorter events, 15.0 us)
Async XLA Ops:
  0.0 40.8 %collective-permute-start.2 = (f32[2,2,128,768]{3,2,1,0:T(8,128)}, f32[2,2,128,768]{3,2,1,0:T(8,128)S(1)}, u32[]{:S(2)}, u32[]{:S(2)}) collective-permute-start(f32[2,2,128,768]{3,2,1,0:T(8,128)} %param.6), channel_id=1, source_target_pairs={{1,0},{2,1},{3,2},{4,3},{5,4},{6,5},{7,6},{8,7},{9,8},{10,9},{11,1... | collective-permute-start | bytes 4718600 | tf_op jit(solution)/shard_map/ppermute | solution.py:12
  22.5 21.3 %collective-permute-start = (f32[2,2,128,768]{3,2,1,0:T(8,128)}, f32[2,2,128,768]{3,2,1,0:T(8,128)S(1)}, u32[]{:S(2)}, u32[]{:S(2)}) collective-permute-start(f32[2,2,128,768]{3,2,1,0:T(8,128)} %param.6), channel_id=1, source_target_pairs={{63,0},{0,1},{1,2},{2,3},{3,4},{4,5},{5,6},{6,7},{7,8},{8,9},{9,10... | collective-permute-start | bytes 4718600 | tf_op jit(solution)/shard_map/ppermute | solution.py:12
  40.8 20.9 %collective-permute-start.3 = (f32[2,2,128,768]{3,2,1,0:T(8,128)S(1)}, f32[2,2,128,768]{3,2,1,0:T(8,128)}, u32[]{:S(2)}, u32[]{:S(2)}) collective-permute-start(f32[2,2,128,768]{3,2,1,0:T(8,128)S(1)} %collective-permute-done.2), channel_id=1, source_target_pairs={{1,0},{2,1},{3,2},{4,3},{5,4},{6,5},{7,6},{8,7},{9,8},{10,9},{11,1... | collective-permute-start | bytes 4718600 | tf_op jit(solution)/shard_map/ppermute | solution.py:12
  43.8 34.8 %copy-start.3 = (f32[2,2,128,768]{3,2,1,0:T(8,128)}, f32[2,2,128,768]{3,2,1,0:T(8,128)S(1)}, u32[]{:S(2)}) copy-start(f32[2,2,128,768]{3,2,1,0:T(8,128)S(1)} %collective-permute-done) | copy-start | bytes 4718596
  43.8 34.8 %collective-permute-start.1 = (f32[2,2,128,768]{3,2,1,0:T(8,128)S(1)}, f32[2,2,128,768]{3,2,1,0:T(8,128)}, u32[]{:S(2)}, u32[]{:S(2)}) collective-permute-start(f32[2,2,128,768]{3,2,1,0:T(8,128)S(1)} %collective-permute-done), channel_id=1, source_target_pairs={{63,0},{0,1},{1,2},{2,3},{3,4},{4,5},{5,6},{6,7},{7,8},{8,9},{9,10... | collective-permute-start | bytes 4718600 | tf_op jit(solution)/shard_map/ppermute | solution.py:12
  61.7 22.0 %collective-permute-start.4 = (f32[2,2,128,768]{3,2,1,0:T(8,128)}, f32[2,2,128,768]{3,2,1,0:T(8,128)}, u32[]{:S(2)}, u32[]{:S(2)}) collective-permute-start(f32[2,2,128,768]{3,2,1,0:T(8,128)} %collective-permute-done.3), channel_id=1, source_target_pairs={{1,0},{2,1},{3,2},{4,3},{5,4},{6,5},{7,6},{8,7},{9,8},{10,9},{11,1... | collective-permute-start | bytes 4718600 | tf_op jit(solution)/shard_map/ppermute | solution.py:12
  66.3 8.4 %copy-start.5 = (f32[512,512]{1,0:T(8,128)S(1)}, f32[512,512]{1,0:T(8,128)}, u32[]{:S(2)}) copy-start(f32[512,512]{1,0:T(8,128)} %param.11) | copy-start | bytes 3145732
  78.6 1.9 copy-start.4
  80.5 1.4 copy-start.1
  83.7 2.1 copy-start.2
  94.5 1.2 copy-start.6
  143.4 46.1 %copy-start = (f32[2,2,768,768]{3,2,1,0:T(8,128)S(1)}, f32[2,2,768,768]{3,2,1,0:T(8,128)}, u32[]{:S(2)}) copy-start(f32[2,2,768,768]{3,2,1,0:T(8,128)} %dynamic_update_slice.3) | copy-start | bytes 28311556
  145.1 21.1 %collective-permute-start.5 = (f32[2,2,128,768]{3,2,1,0:T(8,128)S(1)}, f32[2,2,128,768]{3,2,1,0:T(8,128)S(1)}, u32[]{:S(2)}, u32[]{:S(2)}) collective-permute-start(f32[2,2,128,768]{3,2,1,0:T(8,128)S(1)} %slice.49), channel_id=1, source_target_pairs={{63,0},{0,1},{1,2},{2,3},{3,4},{4,5},{5,6},{6,7},{7,8},{8,9},{9,10... | collective-permute-start | bytes 4718600 | tf_op jit(solution)/shard_map/ppermute | solution.py:12
  168.4 21.1 %collective-permute-start.6 = (f32[2,2,128,768]{3,2,1,0:T(8,128)S(1)}, f32[2,2,128,768]{3,2,1,0:T(8,128)S(1)}, u32[]{:S(2)}, u32[]{:S(2)}) collective-permute-start(f32[2,2,128,768]{3,2,1,0:T(8,128)S(1)} %get-tuple-element.13), channel_id=1, source_target_pairs={{63,0},{0,1},{1,2},{2,3},{3,4},{4,5},{5,6},{6,7},{7,8},{8,9},{9,10... | collective-permute-start | bytes 4718600 | tf_op jit(solution)/shard_map/ppermute | solution.py:12
  168.5 21.0 %collective-permute-start.8 = (f32[2,2,128,768]{3,2,1,0:T(8,128)S(1)}, f32[2,2,128,768]{3,2,1,0:T(8,128)S(1)}, u32[]{:S(2)}, u32[]{:S(2)}) collective-permute-start(f32[2,2,128,768]{3,2,1,0:T(8,128)S(1)} %get-tuple-element.14), channel_id=1, source_target_pairs={{1,0},{2,1},{3,2},{4,3},{5,4},{6,5},{7,6},{8,7},{9,8},{10,9},{11,1... | collective-permute-start | bytes 4718600 | tf_op jit(solution)/shard_map/ppermute | solution.py:12
  189.9 21.1 %collective-permute-start.7 = (f32[2,2,128,768]{3,2,1,0:T(8,128)S(1)}, f32[2,2,128,768]{3,2,1,0:T(8,128)S(1)}, u32[]{:S(2)}, u32[]{:S(2)}) collective-permute-start(f32[2,2,128,768]{3,2,1,0:T(8,128)S(1)} %get-tuple-element.11), channel_id=1, source_target_pairs={{63,0},{0,1},{1,2},{2,3},{3,4},{4,5},{5,6},{6,7},{7,8},{8,9},{9,10... | collective-permute-start | bytes 4718600 | tf_op jit(solution)/shard_map/ppermute | solution.py:12
  190.0 21.0 %collective-permute-start.9 = (f32[2,2,128,768]{3,2,1,0:T(8,128)S(1)}, f32[2,2,128,768]{3,2,1,0:T(8,128)S(1)}, u32[]{:S(2)}, u32[]{:S(2)}) collective-permute-start(f32[2,2,128,768]{3,2,1,0:T(8,128)S(1)} %get-tuple-element.12), channel_id=1, source_target_pairs={{1,0},{2,1},{3,2},{4,3},{5,4},{6,5},{7,6},{8,7},{9,8},{10,9},{11,1... | collective-permute-start | bytes 4718600 | tf_op jit(solution)/shard_map/ppermute | solution.py:12
where the time goes:
time: 214 us; the launch traced here: 213 us
  waiting for transfers between devices  93.3 us (44%)
  local copies, waits for them, and re-layouts  46.4 us (22%)
  starting transfers between devices  34.9 us (16%)
  matrix products  18.9 us (9%)
  other arithmetic  17.3 us (8%)
    ppermute x10, waiting for transfers between devices, shifted(): return lax.ppermute(block, axis, route)  93.3 us
    ppermute x10, starting transfers between devices, shifted(): return lax.ppermute(block, axis, route)  34.9 us
    dynamic_update_slice x1, local copies, waits for them, and re-layouts, body(): lax.dynamic_update_slice(canvas, grads, (anchor, anchor, row_start, col_s...  28.8 us
    unnamed x19, local copies, waits for them, and re-layouts  5.89 us
    dot_general x6, matrix products, transform(): jnp.dot(joined, right_imag, preferred_element_type=jnp.float32)  4.97 us
    dot_general x6, matrix products, transform(): jnp.dot(joined, right_real, preferred_element_type=jnp.float32)  4.94 us
    dot_general x6, matrix products, transform(): jnp.dot(left_real, stacked, preferred_element_type=jnp.float32)  4.52 us
    dot_general x6, matrix products, transform(): jnp.dot(left_imag, stacked, preferred_element_type=jnp.float32)  4.51 us
  transfers between devices with their start and end apart: 10, of which 5 were waited for; matrix products, arithmetic and copies ran while one was open for 7% of the time, Pallas kernels for 0%

commit v1 on v0

v1 whole, which is shorter than its diff:
```python
import functools
import math

import jax
import jax.numpy as jnp
from jax import lax
from jax.experimental import pallas as pl
from jax.experimental.pallas import tpu as pltpu
from jax.sharding import PartitionSpec as P


def hop(block, route):
    size = lax.axis_size("row")
    pairs = [(i, route(i) % size) for i in range(size) if route(i) is not None]
    return lax.ppermute(block, "row", pairs)


def shift(block, distance):
    return hop(block, lambda i: i + distance)


def swap(block):
    return hop(block, lambda i: i ^ 1)


VMEM = pltpu.VMEM
ROWS_AT_ONCE = 128


def cmul(a_real, a_imag, b_real, b_imag):
    return (a_real * b_real - a_imag * b_imag, a_real * b_imag + a_imag * b_real)


def cmul_conj(a_real, a_imag, b_real, b_imag):
    return (a_real * b_real + a_imag * b_imag, a_real * b_imag - a_imag * b_real)


def wave_table(count, step, edge):
    index = lax.broadcasted_iota(jnp.int32, (count, edge), 0) * step
    across = lax.broadcasted_iota(jnp.int32, (count, edge), 1)
    angles = lax.rem(index * across, edge).astype(jnp.float32) * (-2.0 * math.pi / edge)
    return jnp.cos(angles), jnp.sin(angles)


def prepare_kernel(place, probe, left, left_back, right, right_back, light, cos_base, sin_base):
    edge = probe.shape[1]
    fine = 32
    row, col = place[0], place[1]
    factor = 1.0 / math.sqrt(edge)
    fine_cos, fine_sin = wave_table(fine, 1, edge)
    coarse_cos, coarse_sin = wave_table(edge // fine, fine, edge)
    for a in range(edge // fine):
        here = pl.ds(a * fine, fine)
        c, s = coarse_cos[a : a + 1], coarse_sin[a : a + 1]
        rounded = lambda x: (x * factor).astype(jnp.bfloat16).astype(jnp.float32)
        cos_base[here, :] = rounded(c * fine_cos - s * fine_sin)
        sin_base[here, :] = rounded(s * fine_cos + c * fine_sin)
    narrow = lambda x: x.astype(jnp.bfloat16)
    for part, base in enumerate((cos_base, sin_base)):
        here = pl.ds(part * edge, edge)
        left[part] = narrow(pltpu.roll(base[...], row, 1))
        left_back[part] = narrow(pltpu.roll(base[...], row, 0))
        right[here, :] = narrow(pltpu.roll(base[...], col, 0))
        right_back[here, :] = narrow(pltpu.roll(base[...], col, 1))
        light[part] = pltpu.roll(pltpu.roll(probe[part], row, 0), col, 1)


def whole(count):
    return [pl.BlockSpec(memory_space=VMEM)] * count


def prepare(place, probe):
    edge = probe.shape[1]
    pair = jax.ShapeDtypeStruct((2, edge, edge), jnp.bfloat16)
    tall = jax.ShapeDtypeStruct((2 * edge, edge), jnp.bfloat16)
    return pl.pallas_call(
        prepare_kernel,
        in_specs=[pl.BlockSpec(memory_space=pltpu.SMEM)] + whole(1),
        out_specs=whole(5),
        out_shape=[pair, pair, tall, tall, jax.ShapeDtypeStruct(probe.shape, jnp.float32)],
        scratch_shapes=[VMEM((edge, edge), jnp.float32)] * 2,
        compiler_params=pltpu.CompilerParams(vmem_limit_bytes=24 << 20),
        cost_estimate=pl.CostEstimate(flops=16 << 20, bytes_accessed=8 << 20, transcendentals=0),
        name="prepare",
    )(place, probe)


def spectrum(field, left, right, back, emit):
    edge = field.shape[1]
    count = ROWS_AT_ONCE

    @pl.loop(0, edge // count)
    def _(i):
        rows = pl.ds(pl.multiple_of(i * count, count), count)
        c, s = left[0, rows, :], left[1, rows, :]
        if back:
            lhs = [[c, s], [-s, c]]
        else:
            lhs = [[c, -s], [s, c]]
        join = lambda x: jnp.concatenate([jnp.concatenate(y, axis=1) for y in x], axis=0)
        both = jnp.dot(join(lhs), field[...], preferred_element_type=jnp.float32).astype(jnp.bfloat16)
        real, imag = both[:count], both[count:]
        if back:
            lhs = [[real, imag], [imag, -real]]
        else:
            lhs = [[real, -imag], [imag, real]]
        out = jnp.dot(join(lhs), right[...], preferred_element_type=jnp.float32)
        emit(rows, out[:count], out[count:])


def stacked_at(ref, rows):
    return pl.ds(pl.multiple_of(rows.start + ref.shape[1], ROWS_AT_ONCE), rows.size)


def put_field(ref, rows, real, imag):
    ref[rows, :] = real.astype(jnp.bfloat16)
    ref[stacked_at(ref, rows), :] = imag.astype(jnp.bfloat16)


def fill_window(place, own, partner, parts, mult, field, window):
    ahead_top, ahead_bottom, behind, first, second, far = parts
    edge = field.shape[1]
    half = ahead_top.shape[1]
    row, col, even = place[0], place[1], place[2] == 1
    rest = ahead_top.shape[2] - edge
    line = lax.broadcasted_iota(jnp.int32, (half, edge), 0)
    column = lax.broadcasted_iota(jnp.int32, (half, rest), 1)
    top, bottom = pl.ds(0, half), pl.ds(half, half)

    def at(ref, part, where):
        x = ref[part, where, :] if len(ref.shape) == 3 else ref[0, part, where, :]
        return jnp.concatenate(
            [jnp.where(column < col, x[:, edge:], x[:, :rest]), x[:, rest:edge]], axis=1
        )

    def rows_of(q, part):
        pick = lambda a, b: jnp.where(even, a, b)
        if q == 0:
            return jnp.where(line >= row, at(behind, part, bottom), at(ahead_bottom, part, top))
        if q == 1:
            low = pick(at(second, part, top), at(partner, part, top))
            high = pick(at(first, part, top), far[part])
            return jnp.where(line + half >= row, low, high)
        if q == 2:
            return pick(at(second, part, bottom), at(partner, part, bottom))
        if q == 3:
            return at(own, part, top)
        if q == 4:
            return at(own, part, bottom)
        if q == 5:
            return pick(at(partner, part, top), at(first, part, top))
        if q == 6:
            return pick(at(partner, part, bottom), at(second, part, top))
        return at(ahead_top, part, top)

    for q in range(edge // half):
        here = pl.ds(q * half, half)
        real, imag = rows_of(q, 0), rows_of(q, 1)
        if window is not None:
            window[0, here, :] = real
            window[1, here, :] = imag
        out_real, out_imag = cmul(mult[0, here, :], mult[1, here, :], real, imag)
        field[here, :] = out_real.astype(jnp.bfloat16)
        field[pl.ds(edge + q * half, half), :] = out_imag.astype(jnp.bfloat16)


def put_pieces(place, mult, back, send, relay, keep):
    edge = back.shape[1]
    half = relay.shape[1]
    rest = keep.shape[2] - edge
    row, col, even = place[0], place[1], place[2] == 1
    line = lax.broadcasted_iota(jnp.int32, (half, edge), 0)
    column = lax.broadcasted_iota(jnp.int32, (half, edge), 1)
    left, right = pl.ds(0, edge), pl.ds(edge, rest)

    def put(ref, slot, part, value):
        at = pl.ds(slot * half, half) if isinstance(slot, int) else pl.ds(pl.multiple_of(slot * half, half), half)
        ref[part, at, left] = jnp.where(column >= col, value, 0.0)
        ref[part, at, right] = jnp.where(column[:, :rest] < col, value[:, :rest], 0.0)

    by = lambda a, b: jnp.where(even, a, b)
    for q in range(edge // half):
        here = pl.ds(q * half, half)
        grad = cmul_conj(mult[0, here, :], mult[1, here, :], back[0, here, :], back[1, here, :])
        for part, value in enumerate(grad):
            if q == 0:
                put(keep, 4, part, jnp.where(line >= row, value, 0.0))
                put(keep, 3, part, jnp.where(line >= row, 0.0, value))
            elif q == 1:
                high = jnp.where(line + half >= row, 0.0, value)
                relay[part, :, :] = high
                put(send, by(4, 0), part, jnp.where(line + half >= row, value, 0.0))
                put(send, by(2, 4), part, high)
            elif q in (2, 5, 6):
                put(send, {2: by(3, 1), 5: by(0, 2), 6: by(1, 3)}[q], part, value)
            else:
                put(keep, {3: 0, 4: 1, 7: 2}[q], part, value)


def inward_kernel(place, own, partner, a, b, c, d, e, f, light, turn, left, left_back, right, right_back, inner, field, moved):
    fill_window(place, own, partner, (a, b, c, d, e, f), light, field, None)

    def propagate(rows, real, imag):
        put_field(moved, rows, *cmul(real, imag, turn[0, rows, :], turn[1, rows, :]))

    spectrum(field, left, right, False, propagate)

    def store(rows, real, imag):
        inner[0, rows, :] = real
        inner[1, rows, :] = imag

    spectrum(moved, left_back, right_back, True, store)


def turn_kernel(place, own, partner, a, b, c, d, e, f, inner, amplitude, left, left_back, right, right_back, send, relay, keep, mid, field, moved, window, back):
    fill_window(place, own, partner, (a, b, c, d, e, f), inner, field, window)

    def residual(rows, real, imag):
        modulus = jnp.sqrt(real * real + imag * imag)
        scale = 1.0 - amplitude[0, rows, :] / jnp.maximum(modulus, 0.1)
        put_field(moved, rows, real * scale, imag * scale)

    spectrum(field, left, right, False, residual)

    def store(rows, real, imag):
        back[0, rows, :] = real
        back[1, rows, :] = imag
        put_field(mid, rows, *cmul_conj(window[0, rows, :], window[1, rows, :], real, imag))

    spectrum(moved, left_back, right_back, True, store)
    put_pieces(place, inner, back, send, relay, keep)


def outward_kernel(place, mid, light, turn, left, left_back, right, right_back, send, relay, keep, moved, back):
    def propagate(rows, real, imag):
        put_field(moved, rows, *cmul_conj(turn[0, rows, :], turn[1, rows, :], real, imag))

    spectrum(mid, left, right, False, propagate)

    def store(rows, real, imag):
        back[0, rows, :] = real
        back[1, rows, :] = imag

    spectrum(moved, left_back, right_back, True, store)
    put_pieces(place, light, back, send, relay, keep)


def run(kernel, in_specs, arguments, out_shape, scratch):
    return pl.pallas_call(
        kernel,
        grid=(1,),
        in_specs=in_specs,
        out_specs=[pl.BlockSpec(x.shape, functools.partial(lambda n, i: (0,) * n, len(x.shape))) for x in out_shape],
        out_shape=out_shape,
        scratch_shapes=scratch,
        compiler_params=pltpu.CompilerParams(vmem_limit_bytes=36 << 20),
        cost_estimate=pl.CostEstimate(flops=4 << 30, bytes_accessed=16 << 20, transcendentals=0),
    )(*arguments)


def full(x):
    return pl.BlockSpec(x.shape, lambda i: (0,) * x.ndim)


def strip_of(k, x):
    return pl.BlockSpec((1,) + x.shape[1:], lambda i: (k, 0, 0, 0))


def piece_shapes(half, edge, cols):
    wide = jax.ShapeDtypeStruct((2, 5 * half, cols), jnp.float32)
    return [wide, jax.ShapeDtypeStruct((2, half, edge), jnp.float32), wide]


def after(value, *others):
    return lax.optimization_barrier((value,) + others)[0]


def widened(x, start, cols):
    edge = x.shape[2]
    column = lax.broadcasted_iota(jnp.int32, (1, 1, edge), 2)
    rest = cols - edge
    return jnp.concatenate(
        [
            jnp.where(column >= start, x, 0.0),
            jnp.where(column[:, :, :rest] < start, x[:, :, :rest], 0.0),
        ],
        axis=2,
    )


def narrowed(x, start, edge):
    rest = x.shape[2] - edge
    column = lax.broadcasted_iota(jnp.int32, (1, 1, rest), 2)
    return jnp.concatenate(
        [jnp.where(column < start, x[:, :, edge:], x[:, :, :rest]), x[:, :, rest:edge]], axis=2
    )


def scattered(send, relay, keep, even, far_col, then):
    half = relay.shape[1]
    block = lambda x, slot: x[:, slot * half : (slot + 1) * half]
    far = hop(relay, lambda i: i + 1 if i % 2 == 1 else None)
    got = swap(send)
    to_bottom = block(keep, 3) + jnp.where(even, block(got, 3), 0.0)
    to_back = jnp.concatenate(
        [
            jnp.where(even, 0.0, block(got, 4)),
            block(keep, 4) + jnp.where(even, 0.0, block(got, 3)),
        ],
        axis=1,
    )
    far = after(far, to_bottom, to_back)
    to_top = block(keep, 2) + block(got, 2) + widened(far, far_col, keep.shape[2])
    if then is not None:
        to_top, then = lax.optimization_barrier((to_top, then))
    bottom, ahead = shift(to_bottom, 2), shift(to_back, -2)
    top = shift(to_top, 2)
    mine = keep[:, : 2 * half] + got[:, : 2 * half]
    return (mine, ahead, top, bottom), then


def total_of(parts):
    mine, ahead, top, bottom = parts
    return mine + ahead + jnp.concatenate([top, bottom], axis=1)


def body(object_field, row_offset, col_offset, amplitudes, probe, phase):
    strip, cols = object_field.shape[2:]
    half = strip // 2
    edge = probe.shape[1]
    even = lax.rem(lax.axis_index("row"), 2) == 0
    place = jnp.stack([row_offset[0], col_offset[0], even.astype(jnp.int32)])

    lead = lax.optimization_barrier(object_field[0, :, :half])
    rest_field = after(object_field, lead)
    far_col = shift(col_offset, 1)[0]
    top0 = shift(lead, -2)
    bottom0 = shift(rest_field[0, :, half:], -2)
    behind0 = shift(rest_field[0], 2)
    partner = swap(rest_field)
    left, left_back, right, right_back, light = prepare(place, probe)

    carried = lax.optimization_barrier(narrowed(top0, far_col, edge))
    far0 = hop(carried, lambda i: i - 1 if i % 2 == 0 else None)
    first0 = swap(top0)
    later_field, phase = lax.optimization_barrier((rest_field, phase, carried))[:2]
    top1 = shift(later_field[1, :, :half], -2)
    behind1 = shift(after(later_field, bottom0)[1], 2)
    turn = jnp.stack([jnp.cos(phase), jnp.sin(phase)])
    crossing = jnp.where(even, jnp.concatenate([bottom0, bottom0], axis=1), behind0)
    crossing = lax.optimization_barrier(crossing)
    second0 = swap(crossing)
    bottom1 = shift(after(later_field, crossing)[1, :, half:], -2)

    first1 = swap(top1)
    far_col_later, even_later = lax.optimization_barrier((far_col, even, far0, second0))[:2]
    carried = narrowed(top1, far_col_later, edge)
    far1 = hop(carried, lambda i: i - 1 if i % 2 == 0 else None)
    crossing = jnp.where(even_later, jnp.concatenate([bottom1, bottom1], axis=1), behind1)
    second1 = swap(crossing)

    waves = (left, left_back, right, right_back)
    smem = pl.BlockSpec(memory_space=pltpu.SMEM)
    square = jax.ShapeDtypeStruct((2, edge, edge), jnp.float32)
    field = jax.ShapeDtypeStruct((2 * edge, edge), jnp.bfloat16)
    scratch = [VMEM(x.shape, x.dtype) for x in (field, field, square, square)]

    parts = (top0, bottom0, behind0, first0, second0, far0)
    arguments = parts + (light, turn) + waves
    (inner,) = run(
        inward_kernel,
        [smem, strip_of(0, object_field), strip_of(0, partner)] + [full(x) for x in arguments],
        (place, object_field, partner) + arguments,
        [square],
        scratch[:2],
    )

    parts = (top1, bottom1, behind1, first1, second1, far1)
    arguments = parts + (inner, amplitudes) + waves
    send, relay, keep, mid = run(
        turn_kernel,
        [smem, strip_of(1, object_field), strip_of(1, partner)] + [full(x) for x in arguments],
        (place, object_field, partner) + arguments,
        piece_shapes(half, edge, cols) + [field],
        scratch,
    )
    shares2, mid = scattered(send, relay, keep, even, far_col, mid)

    arguments = (mid, light, turn) + waves
    send, relay, keep = run(
        outward_kernel,
        [smem] + [full(x) for x in arguments],
        (place,) + arguments,
        piece_shapes(half, edge, cols),
        [scratch[0], scratch[2]],
    )
    shares1, _ = scattered(send, relay, keep, even, far_col, None)
    return object_field - 0.5 * jnp.stack([total_of(shares1), total_of(shares2)])


def solution(mesh):
    placed = (
        P(None, None, ("scan", "row"), None),
        P(("scan", "row")),
        P(("scan", "row")),
        P(("scan", "row"), None, None),
        P("scan", None, None),
        P(),
    )
    return jax.shard_map(
        body,
        mesh=mesh,
        in_specs=placed,
        out_specs=P(None, None, ("scan", "row"), None),
        check_vma=False,
    )
```

time: 214 us -> 160 us (0.75)
  local copies, waits for them, and re-layouts: 46.4 us -> 12.3 us
  waiting for transfers between devices: 93.3 us -> 60.8 us
  Pallas kernels: 0 us -> 32.1 us
  matrix products: 18.9 us -> 0 us
  other arithmetic: 17.3 us -> 5.05 us
  starting transfers between devices: 34.9 us -> 44.8 us
    ppermute x10 -> x24, waiting for transfers between devices: 93.3 us -> 60.8 us  [hop(): return lax.ppermute(block, 'row', pairs)]
    pallas_call x0 -> x4, Pallas kernels: none -> 32.1 us  [the longest x3 25.5 us: run(): pl.pallas_call(kernel, grid=(1,), in_specs=in_specs, out_specs=[pl.BlockS...]
    dynamic_update_slice x1 -> x0, local copies, waits for them, and re-layouts: 28.8 us -> none  [body(): lax.dynamic_update_slice(canvas, grads, (anchor, anchor, row_start, col_s...]
    dot_general x24 -> x0, matrix products: 18.9 us -> none  [the longest x6 4.97 us: transform(): jnp.dot(joined, right_imag, preferred_element_type=jnp.float32)]
    ppermute x10 -> x24, starting transfers between devices: 34.9 us -> 44.8 us  [hop(): return lax.ppermute(block, 'row', pairs)]
    convert_element_type x3 -> x0, other arithmetic: 6.31 us -> none  [the longest x1 4.39 us: dft_mats(): sin_table = (jnp.sin(angles) * factor).astype(jnp.bfloat16)]
    squeeze x0 -> x6, local copies, waits for them, and re-layouts: none -> 4.95 us  [the longest x1 2.06 us: body(): behind0 = shift(rest_field[0], 2)]
    broadcast_in_dim x1 -> x0, local copies, waits for them, and re-layouts: 4.48 us -> none  [body(): canvas = jnp.zeros(gathered.shape, jnp.float32)]
  transfers between devices with their start and end apart: 10 -> 24, of which waited for: 5 -> 10; matrix products, arithmetic and copies ran while one was open for 7% -> 7% of each run, Pallas kernels for 0% -> 10%
where the time goes in v1:
time: 160 us; the launch traced here: 157 us
  waiting for transfers between devices  60.8 us (38%)
  starting transfers between devices  44.8 us (28%)
  Pallas kernels  32.1 us (20%)
  local copies, waits for them, and re-layouts  12.3 us (8%)
  other arithmetic  5.05 us (3%)
  between operations  1.88 us (1%)
    ppermute x24, waiting for transfers between devices, hop(): return lax.ppermute(block, 'row', pairs)  60.8 us
    ppermute x24, starting transfers between devices, hop(): return lax.ppermute(block, 'row', pairs)  44.8 us
    pallas_call x3, Pallas kernels, run(): pl.pallas_call(kernel, grid=(1,), in_specs=in_specs, out_specs=[pl.BlockS...  25.5 us
    pallas_call x1, Pallas kernels, prepare(): pl.pallas_call(prepare_kernel, in_specs=[pl.BlockSpec(memory_space=pltpu....  6.65 us
    another operation x1, local copies, waits for them, and re-layouts, body(): turn = jnp.stack([jnp.cos(phase), jnp.sin(phase)])  3.69 us
    unnamed x16, local copies, waits for them, and re-layouts  3.63 us
  transfers between devices with their start and end apart: 24, of which 10 were waited for; matrix products, arithmetic and copies ran while one was open for 7% of the time, Pallas kernels for 10%

profile of v1, /device:TPU:38, one launch (start us, length us, event | category | flops | bytes accessed | tf_op | source)
XLA Modules:
  0.0 156.9 jit_solution(14503292503503161877)
XLA Ops:
  0.0 1.8 %slice_bitcast_fusion.5 = f32[2,64,768]{2,1,0:T(8,128)} fusion(f32[2,2,128,768]{3,2,1,0:T(8,128)} %own.3), kind=kLoop, calls=%fused_computation.32 | loop fusion | bytes 786432 | tf_op jit(solution)/shard_map/squeeze | solution.py:334
  1.8 23.0 %collective-permute-start.2 = (f32[2,64,768]{2,1,0:T(8,128)}, f32[2,64,768]{2,1,0:T(8,128)S(1)}, u32[]{:S(2)}, u32[]{:S(2)}) collective-permute-start(f32[2,64,768]{2,1,0:T(8,128)} %slice_bitcast_fusion.5), channel_id=1, source_target_pairs={{0,62},{1,63},{2,0},{3,1},{4,2},{5,3},{6,4},{7,5},{8,6},{9,7},{10,... | collective-permute-start | bytes 1179656 | tf_op jit(solution)/shard_map/ppermute | solution.py:15
  24.8 1.0 slice_bitcast_fusion.3
  25.8 3.5 %collective-permute-start.4 = (f32[2,64,768]{2,1,0:T(8,128)S(1)}, f32[2,64,768]{2,1,0:T(8,128)S(1)}, u32[]{:S(2)}, u32[]{:S(2)}) collective-permute-start(f32[2,64,768]{2,1,0:T(8,128)S(1)} %slice_bitcast_fusion.3), channel_id=1, source_target_pairs={{0,62},{1,63},{2,0},{3,1},{4,2},{5,3},{6,4},{7,5},{8,6},{9,7},{10,... | collective-permute-start | bytes 1179656 | tf_op jit(solution)/shard_map/ppermute | solution.py:15
  29.3 2.1 %slice_bitcast_fusion.1 = f32[2,128,768]{2,1,0:T(8,128)} fusion(f32[2,2,128,768]{3,2,1,0:T(8,128)} %own.3), kind=kLoop, calls=%fused_computation.18 | loop fusion | bytes 1572864 | tf_op jit(solution)/shard_map/squeeze | solution.py:339
  32.9 1.6 %copy-done.1 = f32[2,512,512]{2,1,0:T(8,128)S(1)} copy-done((f32[2,512,512]{2,1,0:T(8,128)S(1)}, f32[2,512,512]{2,1,0:T(8,128)}, u32[]{:S(2)}) %copy-start.1) | copy-done | bytes 2097176
  34.4 6.6 %prepare.1 = (bf16[2,512,512]{2,1,0:T(8,128)(2,1)S(1)}, bf16[2,512,512]{2,1,0:T(8,128)(2,1)S(1)}, bf16[1024,512]{1,0:T(8,128)(2,1)S(1)}, bf16[1024,512]{1,0:T(8,128)(2,1)S(1)}, f32[2,512,512]{2,1,0:T(8,128)S(1)}) custom-call(s32[3]{0:T(128)S(1)} %pad_add_fusion.place, f32[2,512,512]{2,1,0:T(8,128)S(1)} %copy-done.1), custom_call_target="tpu_custom_call" | custom-call | flops 16777216 | bytes 8388608 | tf_op jit(solution)/shard_map/prepare/pallas_call | solution.py:76
  41.7 4.1 %collective-permute-start.9 = (f32[2,64,512]{2,1,0:T(8,128)S(1)}, f32[2,64,512]{2,1,0:T(8,128)S(1)}, u32[]{:S(2)}, u32[]{:S(2)}) collective-permute-start(f32[2,64,512]{2,1,0:T(8,128)S(1)} %pad_maximum_fusion.3), channel_id=1, source_target_pairs={{0,63},{2,1},{4,3},{6,5},{8,7},{10,9},{12,11},{14,13},{16,15},{18,... | collective-permute-start | bytes 786440 | tf_op jit(solution)/shard_map/ppermute | solution.py:15
  46.1 7.1 %collective-permute-done.5.c = f32[2,128,768]{2,1,0:T(8,128)S(1)} collective-permute-done((f32[2,128,768]{2,1,0:T(8,128)}, f32[2,128,768]{2,1,0:T(8,128)S(1)}, u32[]{:S(2)}, u32[]{:S(2)}) %collective-permute-start.5) | collective-permute-done | bytes 786464 | tf_op jit(solution)/shard_map/ppermute | solution.py:15
  54.0 3.7 %cosine_bitcast_fusion = (f32[1,512,512]{2,1,0:T(8,128)S(1)}, f32[1,512,512]{2,1,0:T(8,128)S(1)}) fusion(f32[512,512]{1,0:T(8,128)S(1)} %copy-done.7), kind=kLoop, calls=%fused_computation.4 | loop fusion | bytes 3145728 | tf_op jit(solution)/shard_map/stack | solution.py:349
  57.9 7.8 %collective-permute-done.3.a = f32[2,64,768]{2,1,0:T(8,128)S(1)} collective-permute-done((f32[2,64,768]{2,1,0:T(8,128)S(1)}, f32[2,64,768]{2,1,0:T(8,128)S(1)}, u32[]{:S(2)}, u32[]{:S(2)}) %collective-permute-start.3) | collective-permute-done | bytes 393248 | tf_op jit(solution)/shard_map/ppermute | solution.py:15
  66.2 7.4 %collective-permute-done.6.b = f32[2,64,768]{2,1,0:T(8,128)S(1)} collective-permute-done((f32[2,64,768]{2,1,0:T(8,128)S(1)}, f32[2,64,768]{2,1,0:T(8,128)S(1)}, u32[]{:S(2)}, u32[]{:S(2)}) %collective-permute-start.6) | collective-permute-done | bytes 393248 | tf_op jit(solution)/shard_map/ppermute | solution.py:15
  73.9 0.6 iota_compare_fusion.1
  74.5 3.5 %collective-permute-start.12 = (f32[2,64,512]{2,1,0:T(8,128)S(1)}, f32[2,64,512]{2,1,0:T(8,128)S(1)}, u32[]{:S(2)}, u32[]{:S(2)}) collective-permute-start(f32[2,64,512]{2,1,0:T(8,128)S(1)} %pad_maximum_fusion.4), channel_id=1, source_target_pairs={{0,63},{2,1},{4,3},{6,5},{8,7},{10,9},{12,11},{14,13},{16,15},{18,... | collective-permute-start | bytes 786440 | tf_op jit(solution)/shard_map/ppermute | solution.py:15
  78.1 8.3 %shard_map.64.inner = f32[2,512,512]{2,1,0:T(8,128)S(1)} custom-call(s32[3]{0:T(128)S(1)} %pad_add_fusion.place, f32[2,2,128,768]{3,2,1,0:T(8,128)S(1)} %copy-done, f32[2,2,128,768]{3,2,1,0:T(8,128)} %collective-permute-done.partner, f32[2,64,768]{2,1,0:T(8,128)S(1)} %collective-permute-done.2.a, f32[2,64,768]{2,1,0:T(8,128)S(1)} %collective-permute-done.4.b, ...), custom_call_target="tpu_custom_call" | custom-call | flops 4294967296 | bytes 16777216 | tf_op jit(solution)/shard_map/pallas_call | solution.py:249
  86.5 0.9 copy-done.5
  87.4 1.1 copy-done.6
  88.5 9.5 %shard_map.65 = (f32[2,320,768]{2,1,0:T(8,128)S(1)}, f32[2,64,512]{2,1,0:T(8,128)S(1)}, f32[2,320,768]{2,1,0:T(8,128)S(1)}, bf16[1024,512]{1,0:T(8,128)(2,1)S(1)}) custom-call(s32[3]{0:T(128)S(1)} %pad_add_fusion.place, f32[2,2,128,768]{3,2,1,0:T(8,128)S(1)} %copy-done, f32[2,2,128,768]{3,2,1,0:T(8,128)} %collective-permute-done.partner, ...), custom_call_target="tpu_custom_call" | custom-call | flops 4294967296 | bytes 16777216 | tf_op jit(solution)/shard_map/pallas_call | solution.py:249
  98.2 0.6 compare_reduce_fusion
  99.3 1.3 collective-permute-start.15
  100.6 1.5 collective-permute-done.14
  102.3 5.9 %collective-permute-done.15 = f32[2,64,512]{2,1,0:T(8,128)S(1)} collective-permute-done((f32[2,64,512]{2,1,0:T(8,128)S(1)}, f32[2,64,512]{2,1,0:T(8,128)S(1)}, u32[]{:S(2)}, u32[]{:S(2)}) %collective-permute-start.15) | collective-permute-done | bytes 262176 | tf_op jit(solution)/shard_map/ppermute | solution.py:15
  108.4 7.6 %shard_map.66 = (f32[2,320,768]{2,1,0:T(8,128)S(1)}, f32[2,64,512]{2,1,0:T(8,128)S(1)}, f32[2,320,768]{2,1,0:T(8,128)S(1)}) custom-call(s32[3]{0:T(128)S(1)} %pad_add_fusion.place, bf16[1024,512]{1,0:T(8,128)(2,1)S(1)} %get-tuple-element.45.mid, f32[2,512,512]{2,1,0:T(8,128)S(1)} %get-tuple-element.34.light, f32[2,512,512]{2,1,0:T(8,128)S(1)} %pad_maximum_fusion.turn, ...), custom_call_target="tpu_custom_call" | custom-call | flops 4294967296 | bytes 16777216 | tf_op jit(solution)/shard_map/pallas_call | solution.py:249
  116.3 2.0 %collective-permute-start.23 = (f32[2,64,768]{2,1,0:T(8,128)S(1)}, f32[2,64,768]{2,1,0:T(8,128)S(1)}, u32[]{:S(2)}, u32[]{:S(2)}) collective-permute-start(f32[2,64,768]{2,1,0:T(8,128)S(1)} %get-tuple-element.53), channel_id=1, source_target_pairs={{0,2},{1,3},{2,4},{3,5},{4,6},{5,7},{6,8},{7,9},{8,10},{9,11},{10,... | collective-permute-start | bytes 1179656 | tf_op jit(solution)/shard_map/ppermute | solution.py:15
  118.3 1.3 collective-permute-start.18
  120.3 3.0 %collective-permute-start.17 = (f32[2,128,768]{2,1,0:T(8,128)S(1)}, f32[2,128,768]{2,1,0:T(8,128)S(1)}, u32[]{:S(2)}, u32[]{:S(2)}) collective-permute-start(f32[2,128,768]{2,1,0:T(8,128)S(1)} %pad_maximum_fusion.2), channel_id=1, source_target_pairs={{0,62},{1,63},{2,0},{3,1},{4,2},{5,3},{6,4},{7,5},{8,6},{9,7},{10,... | collective-permute-start | bytes 2359304 | tf_op jit(solution)/shard_map/ppermute | solution.py:15
  123.3 10.3 %collective-permute-done.18 = f32[2,64,512]{2,1,0:T(8,128)S(1)} collective-permute-done((f32[2,64,512]{2,1,0:T(8,128)S(1)}, f32[2,64,512]{2,1,0:T(8,128)S(1)}, u32[]{:S(2)}, u32[]{:S(2)}) %collective-permute-start.18) | collective-permute-done | bytes 262176 | tf_op jit(solution)/shard_map/ppermute | solution.py:15
  133.6 0.7 collective-permute-start.19
  134.4 3.9 %collective-permute-done.22 = f32[2,64,768]{2,1,0:T(8,128)S(1)} collective-permute-done((f32[2,64,768]{2,1,0:T(8,128)S(1)}, f32[2,64,768]{2,1,0:T(8,128)S(1)}, u32[]{:S(2)}, u32[]{:S(2)}) %collective-permute-start.22) | collective-permute-done | bytes 393248 | tf_op jit(solution)/shard_map/ppermute | solution.py:15
  138.9 8.0 %collective-permute-done.19 = f32[2,64,768]{2,1,0:T(8,128)S(1)} collective-permute-done((f32[2,64,768]{2,1,0:T(8,128)S(1)}, f32[2,64,768]{2,1,0:T(8,128)S(1)}, u32[]{:S(2)}, u32[]{:S(2)}) %collective-permute-start.19) | collective-permute-done | bytes 393248 | tf_op jit(solution)/shard_map/ppermute | solution.py:15
  147.0 8.4 %collective-permute-done.20 = f32[2,64,768]{2,1,0:T(8,128)S(1)} collective-permute-done((f32[2,64,768]{2,1,0:T(8,128)S(1)}, f32[2,64,768]{2,1,0:T(8,128)S(1)}, u32[]{:S(2)}, u32[]{:S(2)}) %collective-permute-start.20) | collective-permute-done | bytes 393248 | tf_op jit(solution)/shard_map/ppermute | solution.py:15
  155.6 1.4 fusion
  (68 shorter events, 5.5 us)
Async XLA Ops:
  1.8 39.9 %collective-permute-start.2 = (f32[2,64,768]{2,1,0:T(8,128)}, f32[2,64,768]{2,1,0:T(8,128)S(1)}, u32[]{:S(2)}, u32[]{:S(2)}) collective-permute-start(f32[2,64,768]{2,1,0:T(8,128)} %slice_bitcast_fusion.5), channel_id=1, source_target_pairs={{0,62},{1,63},{2,0},{3,1},{4,2},{5,3},{6,4},{7,5},{8,6},{9,7},{10,... | collective-permute-start | bytes 1179656 | tf_op jit(solution)/shard_map/ppermute | solution.py:15
  24.8 16.3 %collective-permute-start.1 = (s32[1]{0:T(128)}, s32[1]{0:T(128)}, u32[]{:S(2)}, u32[]{:S(2)}) collective-permute-start(s32[1]{0:T(128)} %param.8), channel_id=1, source_target_pairs={{0,1},{1,2},{2,3},{3,4},{4,5},{5,6},{6,7},{7,8},{8,9},{9,10},{10,1... | collective-permute-start | bytes 20 | tf_op jit(solution)/shard_map/ppermute | solution.py:15
  24.8 53.3 %collective-permute-start = (f32[2,2,128,768]{3,2,1,0:T(8,128)}, f32[2,2,128,768]{3,2,1,0:T(8,128)}, u32[]{:S(2)}, u32[]{:S(2)}) collective-permute-start(f32[2,2,128,768]{3,2,1,0:T(8,128)} %own.3), channel_id=1, source_target_pairs={{0,1},{1,0},{2,3},{3,2},{4,5},{5,4},{6,7},{7,6},{8,9},{9,8},{10,11... | collective-permute-start | bytes 4718600 | tf_op jit(solution)/shard_map/ppermute | solution.py:15
  25.8 20.0 %collective-permute-start.4 = (f32[2,64,768]{2,1,0:T(8,128)S(1)}, f32[2,64,768]{2,1,0:T(8,128)S(1)}, u32[]{:S(2)}, u32[]{:S(2)}) collective-permute-start(f32[2,64,768]{2,1,0:T(8,128)S(1)} %slice_bitcast_fusion.3), channel_id=1, source_target_pairs={{0,62},{1,63},{2,0},{3,1},{4,2},{5,3},{6,4},{7,5},{8,6},{9,7},{10,... | collective-permute-start | bytes 1179656 | tf_op jit(solution)/shard_map/ppermute | solution.py:15
  31.3 14.5 %copy-start = (f32[2,2,128,768]{3,2,1,0:T(8,128)S(1)}, f32[2,2,128,768]{3,2,1,0:T(8,128)}, u32[]{:S(2)}) copy-start(f32[2,2,128,768]{3,2,1,0:T(8,128)} %own.3) | copy-start | bytes 4718596
  31.3 21.8 %collective-permute-start.5 = (f32[2,128,768]{2,1,0:T(8,128)}, f32[2,128,768]{2,1,0:T(8,128)S(1)}, u32[]{:S(2)}, u32[]{:S(2)}) collective-permute-start(f32[2,128,768]{2,1,0:T(8,128)} %slice_bitcast_fusion.1), channel_id=1, source_target_pairs={{0,2},{1,3},{2,4},{3,5},{4,6},{5,7},{6,8},{7,9},{8,10},{9,11},{10,... | collective-permute-start | bytes 2359304 | tf_op jit(solution)/shard_map/ppermute | solution.py:15
  32.8 1.6 %copy-start.1 = (f32[2,512,512]{2,1,0:T(8,128)S(1)}, f32[2,512,512]{2,1,0:T(8,128)}, u32[]{:S(2)}) copy-start(f32[2,512,512]{2,1,0:T(8,128)} %probe.1) | copy-start | bytes 6291460
  41.7 12.1 %collective-permute-start.9 = (f32[2,64,512]{2,1,0:T(8,128)S(1)}, f32[2,64,512]{2,1,0:T(8,128)S(1)}, u32[]{:S(2)}, u32[]{:S(2)}) collective-permute-start(f32[2,64,512]{2,1,0:T(8,128)S(1)} %pad_maximum_fusion.3), channel_id=1, source_target_pairs={{0,63},{2,1},{4,3},{6,5},{8,7},{10,9},{12,11},{14,13},{16,15},{18,... | collective-permute-start | bytes 786440 | tf_op jit(solution)/shard_map/ppermute | solution.py:15
  45.9 8.0 %copy-start.7 = (f32[512,512]{1,0:T(8,128)S(1)}, f32[512,512]{1,0:T(8,128)}, u32[]{:S(2)}) copy-start(f32[512,512]{1,0:T(8,128)} %param.11) | copy-start | bytes 3145732
  45.9 27.7 %collective-permute-start.7 = (f32[2,128,768]{2,1,0:T(8,128)S(1)}, f32[2,128,768]{2,1,0:T(8,128)S(1)}, u32[]{:S(2)}, u32[]{:S(2)}) collective-permute-start(f32[2,128,768]{2,1,0:T(8,128)S(1)} %slice_bitcast_fusion), channel_id=1, source_target_pairs={{0,2},{1,3},{2,4},{3,5},{4,6},{5,7},{6,8},{7,9},{8,10},{9,11},{10,... | collective-permute-start | bytes 2359304 | tf_op jit(solution)/shard_map/ppermute | solution.py:15
  53.3 12.5 %collective-permute-start.10 = (f32[2,128,768]{2,1,0:T(8,128)S(1)}, f32[2,128,768]{2,1,0:T(8,128)S(1)}, u32[]{:S(2)}, u32[]{:S(2)}) collective-permute-start(f32[2,128,768]{2,1,0:T(8,128)S(1)} %maximum_select_fusion), channel_id=1, source_target_pairs={{0,1},{1,0},{2,3},{3,2},{4,5},{5,4},{6,7},{7,6},{8,9},{9,8},{10,11... | collective-permute-start | bytes 2359304 | tf_op jit(solution)/shard_map/ppermute | solution.py:15
  53.4 12.3 %collective-permute-start.3 = (f32[2,64,768]{2,1,0:T(8,128)S(1)}, f32[2,64,768]{2,1,0:T(8,128)S(1)}, u32[]{:S(2)}, u32[]{:S(2)}) collective-permute-start(f32[2,64,768]{2,1,0:T(8,128)S(1)} %slice_bitcast_fusion.4), channel_id=1, source_target_pairs={{0,62},{1,63},{2,0},{3,1},{4,2},{5,3},{6,4},{7,5},{8,6},{9,7},{10,... | collective-permute-start | bytes 1179656 | tf_op jit(solution)/shard_map/ppermute | solution.py:15
  53.8 19.9 %collective-permute-start.6 = (f32[2,64,768]{2,1,0:T(8,128)S(1)}, f32[2,64,768]{2,1,0:T(8,128)S(1)}, u32[]{:S(2)}, u32[]{:S(2)}) collective-permute-start(f32[2,64,768]{2,1,0:T(8,128)S(1)} %slice_bitcast_fusion.2), channel_id=1, source_target_pairs={{0,62},{1,63},{2,0},{3,1},{4,2},{5,3},{6,4},{7,5},{8,6},{9,7},{10,... | collective-permute-start | bytes 1179656 | tf_op jit(solution)/shard_map/ppermute | solution.py:15
  65.7 12.3 %collective-permute-start.13 = (f32[2,64,768]{2,1,0:T(8,128)S(1)}, f32[2,64,768]{2,1,0:T(8,128)S(1)}, u32[]{:S(2)}, u32[]{:S(2)}) collective-permute-start(f32[2,64,768]{2,1,0:T(8,128)S(1)} %collective-permute-done.2.a), channel_id=1, source_target_pairs={{0,1},{1,0},{2,3},{3,2},{4,5},{5,4},{6,7},{7,6},{8,9},{9,8},{10,11... | collective-permute-start | bytes 1179656 | tf_op jit(solution)/shard_map/ppermute | solution.py:15
  65.7 20.7 %collective-permute-start.8 = (f32[2,64,768]{2,1,0:T(8,128)S(1)}, f32[2,64,768]{2,1,0:T(8,128)S(1)}, u32[]{:S(2)}, u32[]{:S(2)}) collective-permute-start(f32[2,64,768]{2,1,0:T(8,128)S(1)} %collective-permute-done.3.a), channel_id=1, source_target_pairs={{0,1},{1,0},{2,3},{3,2},{4,5},{5,4},{6,7},{7,6},{8,9},{9,8},{10,11... | collective-permute-start | bytes 1179656 | tf_op jit(solution)/shard_map/ppermute | solution.py:15
  73.7 4.4 %copy-start.2 = (f32[2,128,768]{2,1,0:T(8,128)}, f32[2,128,768]{2,1,0:T(8,128)S(1)}, u32[]{:S(2)}) copy-start(f32[2,128,768]{2,1,0:T(8,128)S(1)} %collective-permute-done.7.c) | copy-start | bytes 2359300
  73.7 12.7 %collective-permute-start.11 = (f32[2,128,768]{2,1,0:T(8,128)S(1)}, f32[2,128,768]{2,1,0:T(8,128)S(1)}, u32[]{:S(2)}, u32[]{:S(2)}) collective-permute-start(f32[2,128,768]{2,1,0:T(8,128)S(1)} %maximum_select_fusion.1), channel_id=1, source_target_pairs={{0,1},{1,0},{2,3},{3,2},{4,5},{5,4},{6,7},{7,6},{8,9},{9,8},{10,11... | collective-permute-start | bytes 2359304 | tf_op jit(solution)/shard_map/ppermute | solution.py:15
  74.5 11.9 %collective-permute-start.12 = (f32[2,64,512]{2,1,0:T(8,128)S(1)}, f32[2,64,512]{2,1,0:T(8,128)S(1)}, u32[]{:S(2)}, u32[]{:S(2)}) collective-permute-start(f32[2,64,512]{2,1,0:T(8,128)S(1)} %pad_maximum_fusion.4), channel_id=1, source_target_pairs={{0,63},{2,1},{4,3},{6,5},{8,7},{10,9},{12,11},{14,13},{16,15},{18,... | collective-permute-start | bytes 786440 | tf_op jit(solution)/shard_map/ppermute | solution.py:15
  78.1 9.3 %copy-start.3 = (f32[2,128,768]{2,1,0:T(8,128)S(1)}, f32[2,128,768]{2,1,0:T(8,128)}, u32[]{:S(2)}) copy-start(f32[2,128,768]{2,1,0:T(8,128)} %copy-done.2) | copy-start | bytes 2359300
  78.1 9.3 %copy-start.4 = (f32[1,512,512]{2,1,0:T(8,128)S(1)}, f32[1,512,512]{2,1,0:T(8,128)}, u32[]{:S(2)}) copy-start(f32[1,512,512]{2,1,0:T(8,128)} %amplitude.1) | copy-start | bytes 3145732
  86.5 0.9 copy-start.5
  87.4 1.1 copy-start.6
  98.0 4.1 %collective-permute-start.14 = (f32[2,320,768]{2,1,0:T(8,128)S(1)}, f32[2,320,768]{2,1,0:T(8,128)S(1)}, u32[]{:S(2)}, u32[]{:S(2)}) collective-permute-start(f32[2,320,768]{2,1,0:T(8,128)S(1)} %get-tuple-element.41), channel_id=1, source_target_pairs={{0,1},{1,0},{2,3},{3,2},{4,5},{5,4},{6,7},{7,6},{8,9},{9,8},{10,11... | collective-permute-start | bytes 5898248 | tf_op jit(solution)/shard_map/ppermute | solution.py:15
  99.3 8.9 %collective-permute-start.15 = (f32[2,64,512]{2,1,0:T(8,128)S(1)}, f32[2,64,512]{2,1,0:T(8,128)S(1)}, u32[]{:S(2)}, u32[]{:S(2)}) collective-permute-start(f32[2,64,512]{2,1,0:T(8,128)S(1)} %get-tuple-element.42), channel_id=1, source_target_pairs={{1,2},{3,4},{5,6},{7,8},{9,10},{11,12},{13,14},{15,16},{17,18},{19... | collective-permute-start | bytes 786440 | tf_op jit(solution)/shard_map/ppermute | solution.py:15
  116.0 4.1 %collective-permute-start.16 = (f32[2,320,768]{2,1,0:T(8,128)S(1)}, f32[2,320,768]{2,1,0:T(8,128)S(1)}, u32[]{:S(2)}, u32[]{:S(2)}) collective-permute-start(f32[2,320,768]{2,1,0:T(8,128)S(1)} %get-tuple-element.47), channel_id=1, source_target_pairs={{0,1},{1,0},{2,3},{3,2},{4,5},{5,4},{6,7},{7,6},{8,9},{9,8},{10,11... | collective-permute-start | bytes 5898248 | tf_op jit(solution)/shard_map/ppermute | solution.py:15
  116.2 22.6 %collective-permute-start.21 = (f32[2,128,768]{2,1,0:T(8,128)S(1)}, f32[2,128,768]{2,1,0:T(8,128)S(1)}, u32[]{:S(2)}, u32[]{:S(2)}) collective-permute-start(f32[2,128,768]{2,1,0:T(8,128)S(1)} %pad_maximum_fusion.1), channel_id=1, source_target_pairs={{0,62},{1,63},{2,0},{3,1},{4,2},{5,3},{6,4},{7,5},{8,6},{9,7},{10,... | collective-permute-start | bytes 2359304 | tf_op jit(solution)/shard_map/ppermute | solution.py:15
  116.3 22.4 %collective-permute-start.23 = (f32[2,64,768]{2,1,0:T(8,128)S(1)}, f32[2,64,768]{2,1,0:T(8,128)S(1)}, u32[]{:S(2)}, u32[]{:S(2)}) collective-permute-start(f32[2,64,768]{2,1,0:T(8,128)S(1)} %get-tuple-element.53), channel_id=1, source_target_pairs={{0,2},{1,3},{2,4},{3,5},{4,6},{5,7},{6,8},{7,9},{8,10},{9,11},{10,... | collective-permute-start | bytes 1179656 | tf_op jit(solution)/shard_map/ppermute | solution.py:15
  118.3 15.2 %collective-permute-start.18 = (f32[2,64,512]{2,1,0:T(8,128)S(1)}, f32[2,64,512]{2,1,0:T(8,128)S(1)}, u32[]{:S(2)}, u32[]{:S(2)}) collective-permute-start(f32[2,64,512]{2,1,0:T(8,128)S(1)} %get-tuple-element.48), channel_id=1, source_target_pairs={{1,2},{3,4},{5,6},{7,8},{9,10},{11,12},{13,14},{15,16},{17,18},{19... | collective-permute-start | bytes 786440 | tf_op jit(solution)/shard_map/ppermute | solution.py:15
  119.6 18.7 %collective-permute-start.22 = (f32[2,64,768]{2,1,0:T(8,128)S(1)}, f32[2,64,768]{2,1,0:T(8,128)S(1)}, u32[]{:S(2)}, u32[]{:S(2)}) collective-permute-start(f32[2,64,768]{2,1,0:T(8,128)S(1)} %fusion.8), channel_id=1, source_target_pairs={{0,2},{1,3},{2,4},{3,5},{4,6},{5,7},{6,8},{7,9},{8,10},{9,11},{10,... | collective-permute-start | bytes 1179656 | tf_op jit(solution)/shard_map/ppermute | solution.py:15
  120.3 35.1 %collective-permute-start.17 = (f32[2,128,768]{2,1,0:T(8,128)S(1)}, f32[2,128,768]{2,1,0:T(8,128)S(1)}, u32[]{:S(2)}, u32[]{:S(2)}) collective-permute-start(f32[2,128,768]{2,1,0:T(8,128)S(1)} %pad_maximum_fusion.2), channel_id=1, source_target_pairs={{0,62},{1,63},{2,0},{3,1},{4,2},{5,3},{6,4},{7,5},{8,6},{9,7},{10,... | collective-permute-start | bytes 2359304 | tf_op jit(solution)/shard_map/ppermute | solution.py:15
  133.6 13.3 %collective-permute-start.19 = (f32[2,64,768]{2,1,0:T(8,128)S(1)}, f32[2,64,768]{2,1,0:T(8,128)S(1)}, u32[]{:S(2)}, u32[]{:S(2)}) collective-permute-start(f32[2,64,768]{2,1,0:T(8,128)S(1)} %fusion.7), channel_id=1, source_target_pairs={{0,2},{1,3},{2,4},{3,5},{4,6},{5,7},{6,8},{7,9},{8,10},{9,11},{10,... | collective-permute-start | bytes 1179656 | tf_op jit(solution)/shard_map/ppermute | solution.py:15
  138.3 17.1 %collective-permute-start.20 = (f32[2,64,768]{2,1,0:T(8,128)S(1)}, f32[2,64,768]{2,1,0:T(8,128)S(1)}, u32[]{:S(2)}, u32[]{:S(2)}) collective-permute-start(f32[2,64,768]{2,1,0:T(8,128)S(1)} %get-tuple-element.51), channel_id=1, source_target_pairs={{0,2},{1,3},{2,4},{3,5},{4,6},{5,7},{6,8},{7,9},{8,10},{9,11},{10,... | collective-permute-start | bytes 1179656 | tf_op jit(solution)/shard_map/ppermute | solution.py:15

commit v2 on v1

--- a/solution.py
+++ b/solution.py
@@ -79,7 +79,7 @@
         out_specs=whole(5),
         out_shape=[pair, pair, tall, tall, jax.ShapeDtypeStruct(probe.shape, jnp.float32)],
         scratch_shapes=[VMEM((edge, edge), jnp.float32)] * 2,
-        compiler_params=pltpu.CompilerParams(vmem_limit_bytes=24 << 20),
+        compiler_params=pltpu.CompilerParams(vmem_limit_bytes=16 << 20),
         cost_estimate=pl.CostEstimate(flops=16 << 20, bytes_accessed=8 << 20, transcendentals=0),
         name="prepare",
     )(place, probe)
@@ -164,7 +164,7 @@
         field[pl.ds(edge + q * half, half), :] = out_imag.astype(jnp.bfloat16)
 
 
-def put_pieces(place, mult, back, send, relay, keep):
+def put_pieces(place, mult, back, send, relay, early, keep):
     edge = back.shape[1]
     half = relay.shape[1]
     rest = keep.shape[2] - edge
@@ -185,7 +185,9 @@
         for part, value in enumerate(grad):
             if q == 0:
                 put(keep, 4, part, jnp.where(line >= row, value, 0.0))
-                put(keep, 3, part, jnp.where(line >= row, 0.0, value))
+                high = jnp.where(line >= row, 0.0, value)
+                put(keep, 3, part, high)
+                early[part, :, :] = high
             elif q == 1:
                 high = jnp.where(line + half >= row, 0.0, value)
                 relay[part, :, :] = high
@@ -212,7 +214,7 @@
     spectrum(moved, left_back, right_back, True, store)
 
 
-def turn_kernel(place, own, partner, a, b, c, d, e, f, inner, amplitude, left, left_back, right, right_back, send, relay, keep, mid, field, moved, window, back):
+def turn_kernel(place, own, partner, a, b, c, d, e, f, inner, amplitude, left, left_back, right, right_back, send, relay, early, keep, mid, field, moved, window, back):
     fill_window(place, own, partner, (a, b, c, d, e, f), inner, field, window)
 
     def residual(rows, real, imag):
@@ -228,10 +230,10 @@
         put_field(mid, rows, *cmul_conj(window[0, rows, :], window[1, rows, :], real, imag))
 
     spectrum(moved, left_back, right_back, True, store)
-    put_pieces(place, inner, back, send, relay, keep)
-
-
-def outward_kernel(place, mid, light, turn, left, left_back, right, right_back, send, relay, keep, moved, back):
+    put_pieces(place, inner, back, send, relay, early, keep)
+
+
+def outward_kernel(place, mid, light, turn, left, left_back, right, right_back, send, relay, early, keep, moved, back):
     def propagate(rows, real, imag):
         put_field(moved, rows, *cmul_conj(turn[0, rows, :], turn[1, rows, :], real, imag))
 
@@ -242,7 +244,7 @@
         back[1, rows, :] = imag
 
     spectrum(moved, left_back, right_back, True, store)
-    put_pieces(place, light, back, send, relay, keep)
+    put_pieces(place, light, back, send, relay, early, keep)
 
 
 def run(kernel, in_specs, arguments, out_shape, scratch):
@@ -253,7 +255,7 @@
         out_specs=[pl.BlockSpec(x.shape, functools.partial(lambda n, i: (0,) * n, len(x.shape))) for x in out_shape],
         out_shape=out_shape,
         scratch_shapes=scratch,
-        compiler_params=pltpu.CompilerParams(vmem_limit_bytes=36 << 20),
+        compiler_params=pltpu.CompilerParams(vmem_limit_bytes=16 << 20),
         cost_estimate=pl.CostEstimate(flops=4 << 30, bytes_accessed=16 << 20, transcendentals=0),
     )(*arguments)
 
@@ -268,7 +270,8 @@
 
 def piece_shapes(half, edge, cols):
     wide = jax.ShapeDtypeStruct((2, 5 * half, cols), jnp.float32)
-    return [wide, jax.ShapeDtypeStruct((2, half, edge), jnp.float32), wide]
+    narrow = jax.ShapeDtypeStruct((2, half, edge), jnp.float32)
+    return [wide, narrow, narrow, wide]
 
 
 def after(value, *others):
@@ -277,31 +280,29 @@
 
 def widened(x, start, cols):
     edge = x.shape[2]
-    column = lax.broadcasted_iota(jnp.int32, (1, 1, edge), 2)
     rest = cols - edge
-    return jnp.concatenate(
-        [
-            jnp.where(column >= start, x, 0.0),
-            jnp.where(column[:, :, :rest] < start, x[:, :, :rest], 0.0),
-        ],
-        axis=2,
-    )
+    column = lax.broadcasted_iota(jnp.int32, x.shape, 2)
+    kept = jnp.where(column >= start, x, 0.0)
+    wrapped = jnp.where(column < start, x, 0.0)[:, :, :rest]
+    return jnp.concatenate([kept, wrapped], axis=2)
 
 
 def narrowed(x, start, edge):
     rest = x.shape[2] - edge
-    column = lax.broadcasted_iota(jnp.int32, (1, 1, rest), 2)
+    column = lax.broadcasted_iota(jnp.int32, x.shape[:2] + (rest,), 2)
     return jnp.concatenate(
         [jnp.where(column < start, x[:, :, edge:], x[:, :, :rest]), x[:, :, rest:edge]], axis=2
     )
 
 
-def scattered(send, relay, keep, even, far_col, then):
+def scattered(send, relay, early, keep, even, far_col, then):
     half = relay.shape[1]
+    cols = keep.shape[2]
     block = lambda x, slot: x[:, slot * half : (slot + 1) * half]
     far = hop(relay, lambda i: i + 1 if i % 2 == 1 else None)
+    early = hop(early, lambda i: i + 2 if i % 2 == 1 else None)
     got = swap(send)
-    to_bottom = block(keep, 3) + jnp.where(even, block(got, 3), 0.0)
+    to_bottom = block(keep, 3) + block(got, 3)
     to_back = jnp.concatenate(
         [
             jnp.where(even, 0.0, block(got, 4)),
@@ -310,17 +311,18 @@
         axis=1,
     )
     far = after(far, to_bottom, to_back)
-    to_top = block(keep, 2) + block(got, 2) + widened(far, far_col, keep.shape[2])
+    to_top = block(keep, 2) + block(got, 2) + widened(far, far_col, cols)
     if then is not None:
         to_top, then = lax.optimization_barrier((to_top, then))
-    bottom, ahead = shift(to_bottom, 2), shift(to_back, -2)
-    top = shift(to_top, 2)
+    late = hop(to_bottom, lambda i: i + 2 if i % 2 == 0 else None)
+    top, ahead = shift(to_top, 2), shift(to_back, -2)
     mine = keep[:, : 2 * half] + got[:, : 2 * half]
-    return (mine, ahead, top, bottom), then
-
-
-def total_of(parts):
-    mine, ahead, top, bottom = parts
+    return (mine, ahead, top, late, early), then
+
+
+def total_of(parts, beyond):
+    mine, ahead, top, late, early = parts
+    bottom = late + widened(early, beyond, mine.shape[2])
     return mine + ahead + jnp.concatenate([top, bottom], axis=1)
 
 
@@ -333,31 +335,26 @@
 
     lead = lax.optimization_barrier(object_field[0, :, :half])
     rest_field = after(object_field, lead)
-    far_col = shift(col_offset, 1)[0]
     top0 = shift(lead, -2)
+    far_col = hop(col_offset, lambda i: i + 1 if i % 2 == 1 else None)[0]
     bottom0 = shift(rest_field[0, :, half:], -2)
     behind0 = shift(rest_field[0], 2)
     partner = swap(rest_field)
-    left, left_back, right, right_back, light = prepare(place, probe)
+    turn = jnp.stack([jnp.cos(phase), jnp.sin(phase)])
 
     carried = lax.optimization_barrier(narrowed(top0, far_col, edge))
     far0 = hop(carried, lambda i: i - 1 if i % 2 == 0 else None)
     first0 = swap(top0)
-    later_field, phase = lax.optimization_barrier((rest_field, phase, carried))[:2]
+    later_field = after(rest_field, carried)
     top1 = shift(later_field[1, :, :half], -2)
-    behind1 = shift(after(later_field, bottom0)[1], 2)
-    turn = jnp.stack([jnp.cos(phase), jnp.sin(phase)])
-    crossing = jnp.where(even, jnp.concatenate([bottom0, bottom0], axis=1), behind0)
-    crossing = lax.optimization_barrier(crossing)
+    bottom1 = shift(later_field[1, :, half:], -2)
+    behind1 = shift(later_field[1], 2)
+    beyond = hop(col_offset, lambda i: i + 2 if i % 2 == 1 else None)[0]
+    left, left_back, right, right_back, light = prepare(place, probe)
+
+    even_after = after(even, light)
+    crossing = jnp.where(even_after, jnp.concatenate([bottom0, bottom0], axis=1), behind0)
     second0 = swap(crossing)
-    bottom1 = shift(after(later_field, crossing)[1, :, half:], -2)
-
-    first1 = swap(top1)
-    far_col_later, even_later = lax.optimization_barrier((far_col, even, far0, second0))[:2]
-    carried = narrowed(top1, far_col_later, edge)
-    far1 = hop(carried, lambda i: i - 1 if i % 2 == 0 else None)
-    crossing = jnp.where(even_later, jnp.concatenate([bottom1, bottom1], axis=1), behind1)
-    second1 = swap(crossing)
 
     waves = (left, left_back, right, right_back)
     smem = pl.BlockSpec(memory_space=pltpu.SMEM)
@@ -375,27 +372,36 @@
         scratch[:2],
     )
 
+    top1_after, even_after = lax.optimization_barrier((top1, even, inner))[:2]
+    carried = narrowed(top1_after, far_col, edge)
+    far1 = hop(carried, lambda i: i - 1 if i % 2 == 0 else None)
+    first1 = swap(top1_after)
+    crossing = jnp.where(even_after, jnp.concatenate([bottom1, bottom1], axis=1), behind1)
+    second1 = swap(crossing)
+
     parts = (top1, bottom1, behind1, first1, second1, far1)
     arguments = parts + (inner, amplitudes) + waves
-    send, relay, keep, mid = run(
+    send, relay, early, keep, mid = run(
         turn_kernel,
         [smem, strip_of(1, object_field), strip_of(1, partner)] + [full(x) for x in arguments],
         (place, object_field, partner) + arguments,
         piece_shapes(half, edge, cols) + [field],
         scratch,
     )
-    shares2, mid = scattered(send, relay, keep, even, far_col, mid)
+    shares2, mid = scattered(send, relay, early, keep, even, far_col, mid)
 
     arguments = (mid, light, turn) + waves
-    send, relay, keep = run(
+    send, relay, early, keep = run(
         outward_kernel,
         [smem] + [full(x) for x in arguments],
         (place,) + arguments,
         piece_shapes(half, edge, cols),
         [scratch[0], scratch[2]],
     )
-    shares1, _ = scattered(send, relay, keep, even, far_col, None)
-    return object_field - 0.5 * jnp.stack([total_of(shares1), total_of(shares2)])
+    shares1, _ = scattered(send, relay, early, keep, even, far_col, None)
+    return object_field - 0.5 * jnp.stack(
+        [total_of(shares1, beyond), total_of(shares2, beyond)]
+    )
 
 
 def solution(mesh):

time: 160 us -> 160 us (level)
  the two profiles are of different devices: /device:TPU:38 before, /device:TPU:37 now
where the time goes in v2:
time: 160 us; the launch traced here: 159 us
  starting transfers between devices  63.2 us (40%)
  waiting for transfers between devices  46 us (29%)
  Pallas kernels  32 us (20%)
  local copies, waits for them, and re-layouts  10.2 us (6%)
  other arithmetic  6.19 us (4%)
  between operations  1.7 us (1%)
    ppermute x27, starting transfers between devices, hop(): return lax.ppermute(block, 'row', pairs)  63.2 us
    ppermute x27, waiting for transfers between devices, hop(): return lax.ppermute(block, 'row', pairs)  46 us
    pallas_call x3, Pallas kernels, run(): pl.pallas_call(kernel, grid=(1,), in_specs=in_specs, out_specs=[pl.BlockS...  25.4 us
    pallas_call x1, Pallas kernels, prepare(): pl.pallas_call(prepare_kernel, in_specs=[pl.BlockSpec(memory_space=pltpu....  6.65 us
    another operation x1, local copies, waits for them, and re-layouts, body(): turn = jnp.stack([jnp.cos(phase), jnp.sin(phase)])  4.49 us
  transfers between devices with their start and end apart: 27, of which 12 were waited for; matrix products, arithmetic and copies ran while one was open for 7% of the time, Pallas kernels for 9%

profile of v2, /device:TPU:37, one launch (start us, length us, event | category | flops | bytes accessed | tf_op | source)
XLA Modules:
  0.0 159.4 jit_solution(4952774069177442482)
XLA Ops:
  1.2 23.7 %collective-permute-start.2 = (f32[2,64,768]{2,1,0:T(8,128)S(1)}, f32[2,64,768]{2,1,0:T(8,128)S(1)}, u32[]{:S(2)}, u32[]{:S(2)}) collective-permute-start(f32[2,64,768]{2,1,0:T(8,128)S(1)} %slice_bitcast_fusion.5), channel_id=1, source_target_pairs={{0,62},{1,63},{2,0},{3,1},{4,2},{5,3},{6,4},{7,5},{8,6},{9,7},{10,... | collective-permute-start | bytes 1179656 | tf_op jit(solution)/shard_map/ppermute | solution.py:15
  25.8 2.1 %slice_bitcast_fusion = f32[2,128,768]{2,1,0:T(8,128)} fusion(f32[2,2,128,768]{3,2,1,0:T(8,128)} %own.3), kind=kLoop, calls=%fused_computation.17 | loop fusion | bytes 1572864 | tf_op jit(solution)/shard_map/squeeze | solution.py:341
  28.6 2.7 %collective-permute-start.6 = (f32[2,64,768]{2,1,0:T(8,128)}, f32[2,64,768]{2,1,0:T(8,128)S(1)}, u32[]{:S(2)}, u32[]{:S(2)}) collective-permute-start(f32[2,64,768]{2,1,0:T(8,128)} %slice_bitcast_fusion.2), channel_id=1, source_target_pairs={{0,62},{1,63},{2,0},{3,1},{4,2},{5,3},{6,4},{7,5},{8,6},{9,7},{10,... | collective-permute-start | bytes 1179656 | tf_op jit(solution)/shard_map/ppermute | solution.py:15
  31.3 1.8 %collective-permute-start.1 = (s32[1]{0:T(128)}, s32[1]{0:T(128)}, u32[]{:S(2)}, u32[]{:S(2)}) collective-permute-start(s32[1]{0:T(128)} %param.8), channel_id=1, source_target_pairs={{1,2},{3,4},{5,6},{7,8},{9,10},{11,12},{13,14},{15,16},{17,18},{19... | collective-permute-start | bytes 20 | tf_op jit(solution)/shard_map/ppermute | solution.py:15
  33.1 4.5 %cosine_bitcast_fusion = (f32[1,512,512]{2,1,0:T(8,128)}, f32[1,512,512]{2,1,0:T(8,128)}) fusion(f32[512,512]{1,0:T(8,128)S(1)} %copy-done.5), kind=kLoop, calls=%fused_computation.4 | loop fusion | bytes 3145728 | tf_op jit(solution)/shard_map/stack | solution.py:343
  39.0 1.6 copy-done.1
  40.6 6.6 %prepare.1 = (bf16[2,512,512]{2,1,0:T(8,128)(2,1)S(1)}, bf16[2,512,512]{2,1,0:T(8,128)(2,1)S(1)}, bf16[1024,512]{1,0:T(8,128)(2,1)S(1)}, bf16[1024,512]{1,0:T(8,128)(2,1)S(1)}, f32[2,512,512]{2,1,0:T(8,128)S(1)}) custom-call(s32[3]{0:T(128)S(1)} %pad_add_fusion.place, f32[2,512,512]{2,1,0:T(8,128)S(1)} %copy-done.1), custom_call_target="tpu_custom_call" | custom-call | flops 16777216 | bytes 8388608 | tf_op jit(solution)/shard_map/prepare/pallas_call | solution.py:76
  48.4 1.4 collective-permute-start.9
  49.8 1.3 collective-permute-start.10
  51.5 3.5 %collective-permute-start.8 = (f32[2,64,768]{2,1,0:T(8,128)S(1)}, f32[2,64,768]{2,1,0:T(8,128)S(1)}, u32[]{:S(2)}, u32[]{:S(2)}) collective-permute-start(f32[2,64,768]{2,1,0:T(8,128)S(1)} %collective-permute-done.2.a), channel_id=1, source_target_pairs={{0,1},{1,0},{2,3},{3,2},{4,5},{5,4},{6,7},{7,6},{8,9},{9,8},{10,11... | collective-permute-start | bytes 1179656 | tf_op jit(solution)/shard_map/ppermute | solution.py:15
  55.2 2.3 %collective-permute-done.10.f = f32[2,64,512]{2,1,0:T(8,128)S(1)} collective-permute-done((f32[2,64,512]{2,1,0:T(8,128)S(1)}, f32[2,64,512]{2,1,0:T(8,128)S(1)}, u32[]{:S(2)}, u32[]{:S(2)}) %collective-permute-start.10) | collective-permute-done | bytes 262176 | tf_op jit(solution)/shard_map/ppermute | solution.py:15
  57.5 3.5 %collective-permute-start.3 = (f32[2,64,768]{2,1,0:T(8,128)S(1)}, f32[2,64,768]{2,1,0:T(8,128)S(1)}, u32[]{:S(2)}, u32[]{:S(2)}) collective-permute-start(f32[2,64,768]{2,1,0:T(8,128)S(1)} %get-tuple-element.58), channel_id=1, source_target_pairs={{0,62},{1,63},{2,0},{3,1},{4,2},{5,3},{6,4},{7,5},{8,6},{9,7},{10,... | collective-permute-start | bytes 1179656 | tf_op jit(solution)/shard_map/ppermute | solution.py:15
  61.1 8.2 %shard_map.64.inner = f32[2,512,512]{2,1,0:T(8,128)S(1)} custom-call(s32[3]{0:T(128)S(1)} %pad_add_fusion.place, f32[2,2,128,768]{3,2,1,0:T(8,128)S(1)} %copy-done, f32[2,2,128,768]{3,2,1,0:T(8,128)} %collective-permute-done.partner, f32[2,64,768]{2,1,0:T(8,128)S(1)} %collective-permute-done.2.a, f32[2,64,768]{2,1,0:T(8,128)S(1)} %collective-permute-done.6.b, ...), custom_call_target="tpu_custom_call" | custom-call | flops 4294967296 | bytes 16777216 | tf_op jit(solution)/shard_map/pallas_call | solution.py:251
  70.0 6.0 %collective-permute-done.4.b = f32[2,64,768]{2,1,0:T(8,128)S(1)} collective-permute-done((f32[2,64,768]{2,1,0:T(8,128)S(1)}, f32[2,64,768]{2,1,0:T(8,128)S(1)}, u32[]{:S(2)}, u32[]{:S(2)}) %collective-permute-start.4) | collective-permute-done | bytes 393248 | tf_op jit(solution)/shard_map/ppermute | solution.py:15
  76.1 1.6 %collective-permute-start.12 = (f32[2,128,768]{2,1,0:T(8,128)S(1)}, f32[2,128,768]{2,1,0:T(8,128)S(1)}, u32[]{:S(2)}, u32[]{:S(2)}) collective-permute-start(f32[2,128,768]{2,1,0:T(8,128)S(1)} %maximum_select_fusion.1), channel_id=1, source_target_pairs={{0,1},{1,0},{2,3},{3,2},{4,5},{5,4},{6,7},{7,6},{8,9},{9,8},{10,11... | collective-permute-start | bytes 2359304 | tf_op jit(solution)/shard_map/ppermute | solution.py:15
  79.2 6.4 %collective-permute-done.13.f = f32[2,64,512]{2,1,0:T(8,128)S(1)} collective-permute-done((f32[2,64,512]{2,1,0:T(8,128)S(1)}, f32[2,64,512]{2,1,0:T(8,128)S(1)}, u32[]{:S(2)}, u32[]{:S(2)}) %collective-permute-start.13) | collective-permute-done | bytes 262176 | tf_op jit(solution)/shard_map/ppermute | solution.py:15
  85.7 9.6 %shard_map.65 = (f32[2,320,768]{2,1,0:T(8,128)S(1)}, f32[2,64,512]{2,1,0:T(8,128)S(1)}, f32[2,64,512]{2,1,0:T(8,128)S(1)}, f32[2,320,768]{2,1,0:T(8,128)S(1)}, bf16[1024,512]{1,0:T(8,128)(2,1)S(1)}) custom-call(s32[3]{0:T(128)S(1)} %pad_add_fusion.place, f32[2,2,128,768]{3,2,1,0:T(8,128)S(1)} %copy-done, f32[2,2,128,768]{3,2,1,0:T(8,128)} %collective-permute-done.partner, ...), custom_call_target="tpu_custom_call" | custom-call | flops 4294967296 | bytes 16777216 | tf_op jit(solution)/shard_map/pallas_call | solution.py:251
  97.1 1.4 collective-permute-start.15
  99.6 2.2 %collective-permute-done.15 = f32[2,64,512]{2,1,0:T(8,128)S(1)} collective-permute-done((f32[2,64,512]{2,1,0:T(8,128)S(1)}, f32[2,64,512]{2,1,0:T(8,128)S(1)}, u32[]{:S(2)}, u32[]{:S(2)}) %collective-permute-start.15) | collective-permute-done | bytes 262176 | tf_op jit(solution)/shard_map/ppermute | solution.py:15
  101.9 7.6 %shard_map.66 = (f32[2,320,768]{2,1,0:T(8,128)S(1)}, f32[2,64,512]{2,1,0:T(8,128)S(1)}, f32[2,64,512]{2,1,0:T(8,128)S(1)}, f32[2,320,768]{2,1,0:T(8,128)S(1)}) custom-call(s32[3]{0:T(128)S(1)} %pad_add_fusion.place, bf16[1024,512]{1,0:T(8,128)(2,1)S(1)} %get-tuple-element.43.mid, f32[2,512,512]{2,1,0:T(8,128)S(1)} %get-tuple-element.30.light, ...), custom_call_target="tpu_custom_call" | custom-call | flops 4294967296 | bytes 16777216 | tf_op jit(solution)/shard_map/pallas_call | solution.py:251
  109.5 4.4 %collective-permute-start.16 = (f32[2,320,768]{2,1,0:T(8,128)S(1)}, f32[2,320,768]{2,1,0:T(8,128)S(1)}, u32[]{:S(2)}, u32[]{:S(2)}) collective-permute-start(f32[2,320,768]{2,1,0:T(8,128)S(1)} %get-tuple-element.45), channel_id=1, source_target_pairs={{0,1},{1,0},{2,3},{3,2},{4,5},{5,4},{6,7},{7,6},{8,9},{9,8},{10,11... | collective-permute-start | bytes 5898248 | tf_op jit(solution)/shard_map/ppermute | solution.py:15
  114.0 1.9 %collective-permute-start.26 = (f32[2,64,512]{2,1,0:T(8,128)S(1)}, f32[2,64,512]{2,1,0:T(8,128)S(1)}, u32[]{:S(2)}, u32[]{:S(2)}) collective-permute-start(f32[2,64,512]{2,1,0:T(8,128)S(1)} %get-tuple-element.50), channel_id=1, source_target_pairs={{1,3},{3,5},{5,7},{7,9},{9,11},{11,13},{13,15},{15,17},{17,19},{19... | collective-permute-start | bytes 786440 | tf_op jit(solution)/shard_map/ppermute | solution.py:15
  115.9 2.0 %collective-permute-start.22 = (f32[2,64,512]{2,1,0:T(8,128)S(1)}, f32[2,64,512]{2,1,0:T(8,128)S(1)}, u32[]{:S(2)}, u32[]{:S(2)}) collective-permute-start(f32[2,64,512]{2,1,0:T(8,128)S(1)} %get-tuple-element.48), channel_id=1, source_target_pairs={{1,3},{3,5},{5,7},{7,9},{9,11},{11,13},{13,15},{15,17},{17,19},{19... | collective-permute-start | bytes 786440 | tf_op jit(solution)/shard_map/ppermute | solution.py:15
  117.9 2.0 %collective-permute-start.21 = (s32[1]{0:T(128)}, s32[1]{0:T(128)}, u32[]{:S(2)}, u32[]{:S(2)}) collective-permute-start(s32[1]{0:T(128)} %param.8), channel_id=1, source_target_pairs={{1,3},{3,5},{5,7},{7,9},{9,11},{11,13},{13,15},{15,17},{17,19},{19... | collective-permute-start | bytes 20 | tf_op jit(solution)/shard_map/ppermute | solution.py:15
  119.8 6.8 %collective-permute-done.21 = s32[1]{0:T(128)} collective-permute-done((s32[1]{0:T(128)}, s32[1]{0:T(128)}, u32[]{:S(2)}, u32[]{:S(2)}) %collective-permute-start.21) | collective-permute-done | bytes 36 | tf_op jit(solution)/shard_map/ppermute | solution.py:15
  129.7 1.3 collective-permute-start.18
  132.9 2.1 %collective-permute-start.17 = (f32[2,128,768]{2,1,0:T(8,128)S(1)}, f32[2,128,768]{2,1,0:T(8,128)S(1)}, u32[]{:S(2)}, u32[]{:S(2)}) collective-permute-start(f32[2,128,768]{2,1,0:T(8,128)S(1)} %pad_maximum_fusion.2), channel_id=1, source_target_pairs={{0,62},{1,63},{2,0},{3,1},{4,2},{5,3},{6,4},{7,5},{8,6},{9,7},{10,... | collective-permute-start | bytes 2359304 | tf_op jit(solution)/shard_map/ppermute | solution.py:15
  136.0 2.1 %collective-permute-start.19 = (f32[2,64,768]{2,1,0:T(8,128)S(1)}, f32[2,64,768]{2,1,0:T(8,128)S(1)}, u32[]{:S(2)}, u32[]{:S(2)}) collective-permute-start(f32[2,64,768]{2,1,0:T(8,128)S(1)} %fusion.7), channel_id=1, source_target_pairs={{0,2},{1,3},{2,4},{3,5},{4,6},{5,7},{6,8},{7,9},{8,10},{9,11},{10,... | collective-permute-start | bytes 1179656 | tf_op jit(solution)/shard_map/ppermute | solution.py:15
  138.1 7.7 %collective-permute-done.24 = f32[2,64,768]{2,1,0:T(8,128)S(1)} collective-permute-done((f32[2,64,768]{2,1,0:T(8,128)S(1)}, f32[2,64,768]{2,1,0:T(8,128)S(1)}, u32[]{:S(2)}, u32[]{:S(2)}) %collective-permute-start.24) | collective-permute-done | bytes 393248 | tf_op jit(solution)/shard_map/ppermute | solution.py:15
  146.1 7.4 %collective-permute-done.19 = f32[2,64,768]{2,1,0:T(8,128)S(1)} collective-permute-done((f32[2,64,768]{2,1,0:T(8,128)S(1)}, f32[2,64,768]{2,1,0:T(8,128)S(1)}, u32[]{:S(2)}, u32[]{:S(2)}) %collective-permute-start.19) | collective-permute-done | bytes 393248 | tf_op jit(solution)/shard_map/ppermute | solution.py:15
  153.5 4.3 %collective-permute-done.17 = f32[2,128,768]{2,1,0:T(8,128)S(1)} collective-permute-done((f32[2,128,768]{2,1,0:T(8,128)S(1)}, f32[2,128,768]{2,1,0:T(8,128)S(1)}, u32[]{:S(2)}, u32[]{:S(2)}) %collective-permute-start.17) | collective-permute-done | bytes 786464 | tf_op jit(solution)/shard_map/ppermute | solution.py:15
  158.0 1.4 fusion
  (74 shorter events, 16.3 us)
Async XLA Ops:
  0.0 27.8 %copy-start = (f32[2,2,128,768]{3,2,1,0:T(8,128)S(1)}, f32[2,2,128,768]{3,2,1,0:T(8,128)}, u32[]{:S(2)}) copy-start(f32[2,2,128,768]{3,2,1,0:T(8,128)} %own.3) | copy-start | bytes 4718596
  0.0 33.1 %copy-start.5 = (f32[512,512]{1,0:T(8,128)S(1)}, f32[512,512]{1,0:T(8,128)}, u32[]{:S(2)}) copy-start(f32[512,512]{1,0:T(8,128)} %param.11) | copy-start | bytes 3145732
  1.2 46.7 %collective-permute-start.2 = (f32[2,64,768]{2,1,0:T(8,128)S(1)}, f32[2,64,768]{2,1,0:T(8,128)S(1)}, u32[]{:S(2)}, u32[]{:S(2)}) collective-permute-start(f32[2,64,768]{2,1,0:T(8,128)S(1)} %slice_bitcast_fusion.5), channel_id=1, source_target_pairs={{0,62},{1,63},{2,0},{3,1},{4,2},{5,3},{6,4},{7,5},{8,6},{9,7},{10,... | collective-permute-start | bytes 1179656 | tf_op jit(solution)/shard_map/ppermute | solution.py:15
  24.9 36.2 %collective-permute-start = (f32[2,2,128,768]{3,2,1,0:T(8,128)}, f32[2,2,128,768]{3,2,1,0:T(8,128)}, u32[]{:S(2)}, u32[]{:S(2)}) collective-permute-start(f32[2,2,128,768]{3,2,1,0:T(8,128)} %own.3), channel_id=1, source_target_pairs={{0,1},{1,0},{2,3},{3,2},{4,5},{5,4},{6,7},{7,6},{8,9},{9,8},{10,11... | collective-permute-start | bytes 4718600 | tf_op jit(solution)/shard_map/ppermute | solution.py:15
  27.8 20.5 %collective-permute-start.7 = (f32[2,128,768]{2,1,0:T(8,128)}, f32[2,128,768]{2,1,0:T(8,128)S(1)}, u32[]{:S(2)}, u32[]{:S(2)}) collective-permute-start(f32[2,128,768]{2,1,0:T(8,128)} %slice_bitcast_fusion), channel_id=1, source_target_pairs={{0,2},{1,3},{2,4},{3,5},{4,6},{5,7},{6,8},{7,9},{8,10},{9,11},{10,... | collective-permute-start | bytes 2359304 | tf_op jit(solution)/shard_map/ppermute | solution.py:15
  28.6 19.3 %collective-permute-start.6 = (f32[2,64,768]{2,1,0:T(8,128)}, f32[2,64,768]{2,1,0:T(8,128)S(1)}, u32[]{:S(2)}, u32[]{:S(2)}) collective-permute-start(f32[2,64,768]{2,1,0:T(8,128)} %slice_bitcast_fusion.2), channel_id=1, source_target_pairs={{0,62},{1,63},{2,0},{3,1},{4,2},{5,3},{6,4},{7,5},{8,6},{9,7},{10,... | collective-permute-start | bytes 1179656 | tf_op jit(solution)/shard_map/ppermute | solution.py:15
  31.3 15.9 %collective-permute-start.1 = (s32[1]{0:T(128)}, s32[1]{0:T(128)}, u32[]{:S(2)}, u32[]{:S(2)}) collective-permute-start(s32[1]{0:T(128)} %param.8), channel_id=1, source_target_pairs={{1,2},{3,4},{5,6},{7,8},{9,10},{11,12},{13,14},{15,16},{17,18},{19... | collective-permute-start | bytes 20 | tf_op jit(solution)/shard_map/ppermute | solution.py:15
  47.9 7.0 %copy-start.3 = (f32[1,512,512]{2,1,0:T(8,128)S(1)}, f32[1,512,512]{2,1,0:T(8,128)}, u32[]{:S(2)}) copy-start(f32[1,512,512]{2,1,0:T(8,128)} %get-tuple-element.59) | copy-start | bytes 3145732
  47.9 7.0 %copy-start.4 = (f32[1,512,512]{2,1,0:T(8,128)S(1)}, f32[1,512,512]{2,1,0:T(8,128)}, u32[]{:S(2)}) copy-start(f32[1,512,512]{2,1,0:T(8,128)} %get-tuple-element.60) | copy-start | bytes 3145732
  48.4 12.6 %collective-permute-start.9 = (f32[2,128,768]{2,1,0:T(8,128)S(1)}, f32[2,128,768]{2,1,0:T(8,128)S(1)}, u32[]{:S(2)}, u32[]{:S(2)}) collective-permute-start(f32[2,128,768]{2,1,0:T(8,128)S(1)} %maximum_select_fusion), channel_id=1, source_target_pairs={{0,1},{1,0},{2,3},{3,2},{4,5},{5,4},{6,7},{7,6},{8,9},{9,8},{10,11... | collective-permute-start | bytes 2359304 | tf_op jit(solution)/shard_map/ppermute | solution.py:15
  49.8 7.7 %collective-permute-start.10 = (f32[2,64,512]{2,1,0:T(8,128)S(1)}, f32[2,64,512]{2,1,0:T(8,128)S(1)}, u32[]{:S(2)}, u32[]{:S(2)}) collective-permute-start(f32[2,64,512]{2,1,0:T(8,128)S(1)} %pad_maximum_fusion.3), channel_id=1, source_target_pairs={{0,63},{2,1},{4,3},{6,5},{8,7},{10,9},{12,11},{14,13},{16,15},{18,... | collective-permute-start | bytes 786440 | tf_op jit(solution)/shard_map/ppermute | solution.py:15
  51.2 24.8 %collective-permute-start.5 = (f32[2,128,768]{2,1,0:T(8,128)S(1)}, f32[2,128,768]{2,1,0:T(8,128)S(1)}, u32[]{:S(2)}, u32[]{:S(2)}) collective-permute-start(f32[2,128,768]{2,1,0:T(8,128)S(1)} %slice_bitcast_fusion.1), channel_id=1, source_target_pairs={{0,2},{1,3},{2,4},{3,5},{4,6},{5,7},{6,8},{7,9},{8,10},{9,11},{10,... | collective-permute-start | bytes 2359304 | tf_op jit(solution)/shard_map/ppermute | solution.py:15
  51.5 9.5 %collective-permute-start.8 = (f32[2,64,768]{2,1,0:T(8,128)S(1)}, f32[2,64,768]{2,1,0:T(8,128)S(1)}, u32[]{:S(2)}, u32[]{:S(2)}) collective-permute-start(f32[2,64,768]{2,1,0:T(8,128)S(1)} %collective-permute-done.2.a), channel_id=1, source_target_pairs={{0,1},{1,0},{2,3},{3,2},{4,5},{5,4},{6,7},{7,6},{8,9},{9,8},{10,11... | collective-permute-start | bytes 1179656 | tf_op jit(solution)/shard_map/ppermute | solution.py:15
  57.5 12.4 %collective-permute-start.3 = (f32[2,64,768]{2,1,0:T(8,128)S(1)}, f32[2,64,768]{2,1,0:T(8,128)S(1)}, u32[]{:S(2)}, u32[]{:S(2)}) collective-permute-start(f32[2,64,768]{2,1,0:T(8,128)S(1)} %get-tuple-element.58), channel_id=1, source_target_pairs={{0,62},{1,63},{2,0},{3,1},{4,2},{5,3},{6,4},{7,5},{8,6},{9,7},{10,... | collective-permute-start | bytes 1179656 | tf_op jit(solution)/shard_map/ppermute | solution.py:15
  61.0 14.9 %collective-permute-start.4 = (f32[2,64,768]{2,1,0:T(8,128)S(1)}, f32[2,64,768]{2,1,0:T(8,128)S(1)}, u32[]{:S(2)}, u32[]{:S(2)}) collective-permute-start(f32[2,64,768]{2,1,0:T(8,128)S(1)} %get-tuple-element.57), channel_id=1, source_target_pairs={{0,62},{1,63},{2,0},{3,1},{4,2},{5,3},{6,4},{7,5},{8,6},{9,7},{10,... | collective-permute-start | bytes 1179656 | tf_op jit(solution)/shard_map/ppermute | solution.py:15
  69.3 16.4 %copy-start.2 = (f32[1,512,512]{2,1,0:T(8,128)S(1)}, f32[1,512,512]{2,1,0:T(8,128)}, u32[]{:S(2)}) copy-start(f32[1,512,512]{2,1,0:T(8,128)} %amplitude.1) | copy-start | bytes 3145732
  76.1 9.6 %collective-permute-start.12 = (f32[2,128,768]{2,1,0:T(8,128)S(1)}, f32[2,128,768]{2,1,0:T(8,128)S(1)}, u32[]{:S(2)}, u32[]{:S(2)}) collective-permute-start(f32[2,128,768]{2,1,0:T(8,128)S(1)} %maximum_select_fusion.1), channel_id=1, source_target_pairs={{0,1},{1,0},{2,3},{3,2},{4,5},{5,4},{6,7},{7,6},{8,9},{9,8},{10,11... | collective-permute-start | bytes 2359304 | tf_op jit(solution)/shard_map/ppermute | solution.py:15
  77.7 7.9 %collective-permute-start.11 = (f32[2,64,768]{2,1,0:T(8,128)S(1)}, f32[2,64,768]{2,1,0:T(8,128)S(1)}, u32[]{:S(2)}, u32[]{:S(2)}) collective-permute-start(f32[2,64,768]{2,1,0:T(8,128)S(1)} %collective-permute-done.3.a), channel_id=1, source_target_pairs={{0,1},{1,0},{2,3},{3,2},{4,5},{5,4},{6,7},{7,6},{8,9},{9,8},{10,11... | collective-permute-start | bytes 1179656 | tf_op jit(solution)/shard_map/ppermute | solution.py:15
  77.9 7.7 %collective-permute-start.13 = (f32[2,64,512]{2,1,0:T(8,128)S(1)}, f32[2,64,512]{2,1,0:T(8,128)S(1)}, u32[]{:S(2)}, u32[]{:S(2)}) collective-permute-start(f32[2,64,512]{2,1,0:T(8,128)S(1)} %pad_maximum_fusion.4), channel_id=1, source_target_pairs={{0,63},{2,1},{4,3},{6,5},{8,7},{10,9},{12,11},{14,13},{16,15},{18,... | collective-permute-start | bytes 786440 | tf_op jit(solution)/shard_map/ppermute | solution.py:15
  95.2 4.2 %collective-permute-start.14 = (f32[2,320,768]{2,1,0:T(8,128)S(1)}, f32[2,320,768]{2,1,0:T(8,128)S(1)}, u32[]{:S(2)}, u32[]{:S(2)}) collective-permute-start(f32[2,320,768]{2,1,0:T(8,128)S(1)} %get-tuple-element.39), channel_id=1, source_target_pairs={{0,1},{1,0},{2,3},{3,2},{4,5},{5,4},{6,7},{7,6},{8,9},{9,8},{10,11... | collective-permute-start | bytes 5898248 | tf_op jit(solution)/shard_map/ppermute | solution.py:15
  97.1 4.7 %collective-permute-start.15 = (f32[2,64,512]{2,1,0:T(8,128)S(1)}, f32[2,64,512]{2,1,0:T(8,128)S(1)}, u32[]{:S(2)}, u32[]{:S(2)}) collective-permute-start(f32[2,64,512]{2,1,0:T(8,128)S(1)} %get-tuple-element.40), channel_id=1, source_target_pairs={{1,2},{3,4},{5,6},{7,8},{9,10},{11,12},{13,14},{15,16},{17,18},{19... | collective-permute-start | bytes 786440 | tf_op jit(solution)/shard_map/ppermute | solution.py:15
  109.5 22.5 %collective-permute-start.16 = (f32[2,320,768]{2,1,0:T(8,128)S(1)}, f32[2,320,768]{2,1,0:T(8,128)S(1)}, u32[]{:S(2)}, u32[]{:S(2)}) collective-permute-start(f32[2,320,768]{2,1,0:T(8,128)S(1)} %get-tuple-element.45), channel_id=1, source_target_pairs={{0,1},{1,0},{2,3},{3,2},{4,5},{5,4},{6,7},{7,6},{8,9},{9,8},{10,11... | collective-permute-start | bytes 5898248 | tf_op jit(solution)/shard_map/ppermute | solution.py:15
  114.0 15.8 %collective-permute-start.26 = (f32[2,64,512]{2,1,0:T(8,128)S(1)}, f32[2,64,512]{2,1,0:T(8,128)S(1)}, u32[]{:S(2)}, u32[]{:S(2)}) collective-permute-start(f32[2,64,512]{2,1,0:T(8,128)S(1)} %get-tuple-element.50), channel_id=1, source_target_pairs={{1,3},{3,5},{5,7},{7,9},{9,11},{11,13},{13,15},{15,17},{17,19},{19... | collective-permute-start | bytes 786440 | tf_op jit(solution)/shard_map/ppermute | solution.py:15
  115.9 15.2 %collective-permute-start.22 = (f32[2,64,512]{2,1,0:T(8,128)S(1)}, f32[2,64,512]{2,1,0:T(8,128)S(1)}, u32[]{:S(2)}, u32[]{:S(2)}) collective-permute-start(f32[2,64,512]{2,1,0:T(8,128)S(1)} %get-tuple-element.48), channel_id=1, source_target_pairs={{1,3},{3,5},{5,7},{7,9},{9,11},{11,13},{13,15},{15,17},{17,19},{19... | collective-permute-start | bytes 786440 | tf_op jit(solution)/shard_map/ppermute | solution.py:15
  117.9 8.8 %collective-permute-start.21 = (s32[1]{0:T(128)}, s32[1]{0:T(128)}, u32[]{:S(2)}, u32[]{:S(2)}) collective-permute-start(s32[1]{0:T(128)} %param.8), channel_id=1, source_target_pairs={{1,3},{3,5},{5,7},{7,9},{9,11},{11,13},{13,15},{15,17},{17,19},{19... | collective-permute-start | bytes 20 | tf_op jit(solution)/shard_map/ppermute | solution.py:15
  128.0 4.0 %collective-permute-start.25 = (f32[2,64,768]{2,1,0:T(8,128)S(1)}, f32[2,64,768]{2,1,0:T(8,128)S(1)}, u32[]{:S(2)}, u32[]{:S(2)}) collective-permute-start(f32[2,64,768]{2,1,0:T(8,128)S(1)} %get-tuple-element.53), channel_id=1, source_target_pairs={{0,2},{2,4},{4,6},{6,8},{8,10},{10,12},{12,14},{14,16},{16,18},{18... | collective-permute-start | bytes 1179656 | tf_op jit(solution)/shard_map/ppermute | solution.py:15
  128.6 17.1 %collective-permute-start.23 = (f32[2,128,768]{2,1,0:T(8,128)S(1)}, f32[2,128,768]{2,1,0:T(8,128)S(1)}, u32[]{:S(2)}, u32[]{:S(2)}) collective-permute-start(f32[2,128,768]{2,1,0:T(8,128)S(1)} %pad_maximum_fusion.1), channel_id=1, source_target_pairs={{0,62},{1,63},{2,0},{3,1},{4,2},{5,3},{6,4},{7,5},{8,6},{9,7},{10,... | collective-permute-start | bytes 2359304 | tf_op jit(solution)/shard_map/ppermute | solution.py:15
  129.7 6.1 %collective-permute-start.18 = (f32[2,64,512]{2,1,0:T(8,128)S(1)}, f32[2,64,512]{2,1,0:T(8,128)S(1)}, u32[]{:S(2)}, u32[]{:S(2)}) collective-permute-start(f32[2,64,512]{2,1,0:T(8,128)S(1)} %get-tuple-element.46), channel_id=1, source_target_pairs={{1,2},{3,4},{5,6},{7,8},{9,10},{11,12},{13,14},{15,16},{17,18},{19... | collective-permute-start | bytes 786440 | tf_op jit(solution)/shard_map/ppermute | solution.py:15
  131.1 14.7 %collective-permute-start.24 = (f32[2,64,768]{2,1,0:T(8,128)S(1)}, f32[2,64,768]{2,1,0:T(8,128)S(1)}, u32[]{:S(2)}, u32[]{:S(2)}) collective-permute-start(f32[2,64,768]{2,1,0:T(8,128)S(1)} %fusion.8), channel_id=1, source_target_pairs={{0,2},{1,3},{2,4},{3,5},{4,6},{5,7},{6,8},{7,9},{8,10},{9,11},{10,... | collective-permute-start | bytes 1179656 | tf_op jit(solution)/shard_map/ppermute | solution.py:15
  132.2 13.9 %collective-permute-start.20 = (f32[2,64,768]{2,1,0:T(8,128)S(1)}, f32[2,64,768]{2,1,0:T(8,128)S(1)}, u32[]{:S(2)}, u32[]{:S(2)}) collective-permute-start(f32[2,64,768]{2,1,0:T(8,128)S(1)} %get-tuple-element.51), channel_id=1, source_target_pairs={{0,2},{2,4},{4,6},{6,8},{8,10},{10,12},{12,14},{14,16},{16,18},{18... | collective-permute-start | bytes 1179656 | tf_op jit(solution)/shard_map/ppermute | solution.py:15
  132.9 24.8 %collective-permute-start.17 = (f32[2,128,768]{2,1,0:T(8,128)S(1)}, f32[2,128,768]{2,1,0:T(8,128)S(1)}, u32[]{:S(2)}, u32[]{:S(2)}) collective-permute-start(f32[2,128,768]{2,1,0:T(8,128)S(1)} %pad_maximum_fusion.2), channel_id=1, source_target_pairs={{0,62},{1,63},{2,0},{3,1},{4,2},{5,3},{6,4},{7,5},{8,6},{9,7},{10,... | collective-permute-start | bytes 2359304 | tf_op jit(solution)/shard_map/ppermute | solution.py:15
  136.0 17.5 %collective-permute-start.19 = (f32[2,64,768]{2,1,0:T(8,128)S(1)}, f32[2,64,768]{2,1,0:T(8,128)S(1)}, u32[]{:S(2)}, u32[]{:S(2)}) collective-permute-start(f32[2,64,768]{2,1,0:T(8,128)S(1)} %fusion.7), channel_id=1, source_target_pairs={{0,2},{1,3},{2,4},{3,5},{4,6},{5,7},{6,8},{7,9},{8,10},{9,11},{10,... | collective-permute-start | bytes 1179656 | tf_op jit(solution)/shard_map/ppermute | solution.py:15
  (1 other events, 1.6 us)

commit v3 on v2

--- a/solution.py
+++ b/solution.py
@@ -118,9 +118,12 @@
 
 
 def fill_window(place, own, partner, parts, mult, field, window):
-    ahead_top, ahead_bottom, behind, first, second, far = parts
+    ahead_top, ahead_bottom, behind, swapped, far = parts
     edge = field.shape[1]
-    half = ahead_top.shape[1]
+    half = far.shape[1]
+    if ahead_bottom is None:
+        ahead_top, ahead_bottom = (ahead_top.at[:, pl.ds(i * half, half), :] for i in range(2))
+    first, second = swapped.at[:, pl.ds(0, half), :], swapped.at[:, pl.ds(half, 2 * half), :]
     row, col, even = place[0], place[1], place[2] == 1
     rest = ahead_top.shape[2] - edge
     line = lax.broadcasted_iota(jnp.int32, (half, edge), 0)
@@ -164,7 +167,7 @@
         field[pl.ds(edge + q * half, half), :] = out_imag.astype(jnp.bfloat16)
 
 
-def put_pieces(place, mult, back, send, relay, early, keep):
+def put_pieces(place, mult, back, send, relay, keep):
     edge = back.shape[1]
     half = relay.shape[1]
     rest = keep.shape[2] - edge
@@ -185,9 +188,7 @@
         for part, value in enumerate(grad):
             if q == 0:
                 put(keep, 4, part, jnp.where(line >= row, value, 0.0))
-                high = jnp.where(line >= row, 0.0, value)
-                put(keep, 3, part, high)
-                early[part, :, :] = high
+                put(keep, 3, part, jnp.where(line >= row, 0.0, value))
             elif q == 1:
                 high = jnp.where(line + half >= row, 0.0, value)
                 relay[part, :, :] = high
@@ -199,8 +200,8 @@
                 put(keep, {3: 0, 4: 1, 7: 2}[q], part, value)
 
 
-def inward_kernel(place, own, partner, a, b, c, d, e, f, light, turn, left, left_back, right, right_back, inner, field, moved):
-    fill_window(place, own, partner, (a, b, c, d, e, f), light, field, None)
+def inward_kernel(place, own, partner, ahead, behind, swapped, far, light, turn, left, left_back, right, right_back, inner, field, moved):
+    fill_window(place, own, partner, (ahead, None, behind, swapped, far), light, field, None)
 
     def propagate(rows, real, imag):
         put_field(moved, rows, *cmul(real, imag, turn[0, rows, :], turn[1, rows, :]))
@@ -214,8 +215,8 @@
     spectrum(moved, left_back, right_back, True, store)
 
 
-def turn_kernel(place, own, partner, a, b, c, d, e, f, inner, amplitude, left, left_back, right, right_back, send, relay, early, keep, mid, field, moved, window, back):
-    fill_window(place, own, partner, (a, b, c, d, e, f), inner, field, window)
+def turn_kernel(place, own, partner, top, bottom, behind, swapped, far, inner, amplitude, left, left_back, right, right_back, send, relay, keep, mid, field, moved, window, back):
+    fill_window(place, own, partner, (top, bottom, behind, swapped, far), inner, field, window)
 
     def residual(rows, real, imag):
         modulus = jnp.sqrt(real * real + imag * imag)
@@ -230,10 +231,10 @@
         put_field(mid, rows, *cmul_conj(window[0, rows, :], window[1, rows, :], real, imag))
 
     spectrum(moved, left_back, right_back, True, store)
-    put_pieces(place, inner, back, send, relay, early, keep)
-
-
-def outward_kernel(place, mid, light, turn, left, left_back, right, right_back, send, relay, early, keep, moved, back):
+    put_pieces(place, inner, back, send, relay, keep)
+
+
+def outward_kernel(place, mid, light, turn, left, left_back, right, right_back, send, relay, keep, moved, back):
     def propagate(rows, real, imag):
         put_field(moved, rows, *cmul_conj(turn[0, rows, :], turn[1, rows, :], real, imag))
 
@@ -244,7 +245,7 @@
         back[1, rows, :] = imag
 
     spectrum(moved, left_back, right_back, True, store)
-    put_pieces(place, light, back, send, relay, early, keep)
+    put_pieces(place, light, back, send, relay, keep)
 
 
 def run(kernel, in_specs, arguments, out_shape, scratch):
@@ -271,7 +272,7 @@
 def piece_shapes(half, edge, cols):
     wide = jax.ShapeDtypeStruct((2, 5 * half, cols), jnp.float32)
     narrow = jax.ShapeDtypeStruct((2, half, edge), jnp.float32)
-    return [wide, narrow, narrow, wide]
+    return [wide, narrow, wide]
 
 
 def after(value, *others):
@@ -295,14 +296,12 @@
     )
 
 
-def scattered(send, relay, early, keep, even, far_col, then):
+def scattered(send, relay, keep, even, far_col, then):
     half = relay.shape[1]
-    cols = keep.shape[2]
     block = lambda x, slot: x[:, slot * half : (slot + 1) * half]
     far = hop(relay, lambda i: i + 1 if i % 2 == 1 else None)
-    early = hop(early, lambda i: i + 2 if i % 2 == 1 else None)
     got = swap(send)
-    to_bottom = block(keep, 3) + block(got, 3)
+    to_bottom = block(keep, 3) + jnp.where(even, block(got, 3), 0.0)
     to_back = jnp.concatenate(
         [
             jnp.where(even, 0.0, block(got, 4)),
@@ -310,20 +309,16 @@
         ],
         axis=1,
     )
-    far = after(far, to_bottom, to_back)
-    to_top = block(keep, 2) + block(got, 2) + widened(far, far_col, cols)
+    mine = keep[:, : 2 * half] + got[:, : 2 * half]
+    to_top = lambda far: block(keep, 2) + block(got, 2) + widened(far, far_col, keep.shape[2])
     if then is not None:
-        to_top, then = lax.optimization_barrier((to_top, then))
-    late = hop(to_bottom, lambda i: i + 2 if i % 2 == 0 else None)
-    top, ahead = shift(to_top, 2), shift(to_back, -2)
-    mine = keep[:, : 2 * half] + got[:, : 2 * half]
-    return (mine, ahead, top, late, early), then
-
-
-def total_of(parts, beyond):
-    mine, ahead, top, late, early = parts
-    bottom = late + widened(early, beyond, mine.shape[2])
-    return mine + ahead + jnp.concatenate([top, bottom], axis=1)
+        to_ahead, then = lax.optimization_barrier((jnp.concatenate([to_top(far), to_bottom], axis=1), then))
+        ahead = shift(to_ahead, 2)
+    else:
+        top = to_top(after(far, to_bottom, to_back))
+        ahead = [shift(to_bottom, 2)]
+        ahead = jnp.concatenate([shift(top, 2)] + ahead, axis=1)
+    return mine + shift(to_back, -2) + ahead, then
 
 
 def body(object_field, row_offset, col_offset, amplitudes, probe, phase):
@@ -333,28 +328,28 @@
     even = lax.rem(lax.axis_index("row"), 2) == 0
     place = jnp.stack([row_offset[0], col_offset[0], even.astype(jnp.int32)])
 
-    lead = lax.optimization_barrier(object_field[0, :, :half])
+    lead = lax.optimization_barrier(object_field[0])
     rest_field = after(object_field, lead)
-    top0 = shift(lead, -2)
+    ahead0 = shift(lead, -2)
     far_col = hop(col_offset, lambda i: i + 1 if i % 2 == 1 else None)[0]
-    bottom0 = shift(rest_field[0, :, half:], -2)
-    behind0 = shift(rest_field[0], 2)
+    behind0 = shift(lead, 2)
     partner = swap(rest_field)
     turn = jnp.stack([jnp.cos(phase), jnp.sin(phase)])
-
-    carried = lax.optimization_barrier(narrowed(top0, far_col, edge))
+    left, left_back, right, right_back, light = prepare(place, probe)
+
+    def crossing(ahead, behind, even):
+        top, bottom = ahead
+        return jnp.concatenate(
+            [top, jnp.where(even, jnp.concatenate([bottom, bottom], axis=1), behind)], axis=1
+        )
+
+    carried = lax.optimization_barrier(narrowed(ahead0[:, :half], far_col, edge))
     far0 = hop(carried, lambda i: i - 1 if i % 2 == 0 else None)
-    first0 = swap(top0)
-    later_field = after(rest_field, carried)
+    later_field = after(rest_field, light)
     top1 = shift(later_field[1, :, :half], -2)
     bottom1 = shift(later_field[1, :, half:], -2)
     behind1 = shift(later_field[1], 2)
-    beyond = hop(col_offset, lambda i: i + 2 if i % 2 == 1 else None)[0]
-    left, left_back, right, right_back, light = prepare(place, probe)
-
-    even_after = after(even, light)
-    crossing = jnp.where(even_after, jnp.concatenate([bottom0, bottom0], axis=1), behind0)
-    second0 = swap(crossing)
+    swapped0 = swap(crossing((ahead0[:, :half], ahead0[:, half:]), behind0, after(even, carried)))
 
     waves = (left, left_back, right, right_back)
     smem = pl.BlockSpec(memory_space=pltpu.SMEM)
@@ -362,7 +357,7 @@
     field = jax.ShapeDtypeStruct((2 * edge, edge), jnp.bfloat16)
     scratch = [VMEM(x.shape, x.dtype) for x in (field, field, square, square)]
 
-    parts = (top0, bottom0, behind0, first0, second0, far0)
+    parts = (ahead0, behind0, swapped0, far0)
     arguments = parts + (light, turn) + waves
     (inner,) = run(
         inward_kernel,
@@ -375,33 +370,29 @@
     top1_after, even_after = lax.optimization_barrier((top1, even, inner))[:2]
     carried = narrowed(top1_after, far_col, edge)
     far1 = hop(carried, lambda i: i - 1 if i % 2 == 0 else None)
-    first1 = swap(top1_after)
-    crossing = jnp.where(even_after, jnp.concatenate([bottom1, bottom1], axis=1), behind1)
-    second1 = swap(crossing)
-
-    parts = (top1, bottom1, behind1, first1, second1, far1)
+    swapped1 = swap(crossing((top1_after, bottom1), behind1, even_after))
+
+    parts = (top1, bottom1, behind1, swapped1, far1)
     arguments = parts + (inner, amplitudes) + waves
-    send, relay, early, keep, mid = run(
+    send, relay, keep, mid = run(
         turn_kernel,
         [smem, strip_of(1, object_field), strip_of(1, partner)] + [full(x) for x in arguments],
         (place, object_field, partner) + arguments,
         piece_shapes(half, edge, cols) + [field],
         scratch,
     )
-    shares2, mid = scattered(send, relay, early, keep, even, far_col, mid)
+    total2, mid = scattered(send, relay, keep, even, far_col, mid)
 
     arguments = (mid, light, turn) + waves
-    send, relay, early, keep = run(
+    send, relay, keep = run(
         outward_kernel,
         [smem] + [full(x) for x in arguments],
         (place,) + arguments,
         piece_shapes(half, edge, cols),
         [scratch[0], scratch[2]],
     )
-    shares1, _ = scattered(send, relay, early, keep, even, far_col, None)
-    return object_field - 0.5 * jnp.stack(
-        [total_of(shares1, beyond), total_of(shares2, beyond)]
-    )
+    total1, _ = scattered(send, relay, keep, even, far_col, None)
+    return object_field - 0.5 * jnp.stack([total1, total2])
 
 
 def solution(mesh):

time: 160 us -> 160 us (level)
  the two profiles are of different devices: /device:TPU:37 before, /device:TPU:38 now
where the time goes in v3:
time: 160 us; the launch traced here: 158 us
  waiting for transfers between devices  67.8 us (42%)
  starting transfers between devices  43.2 us (27%)
  Pallas kernels  32.4 us (20%)
  local copies, waits for them, and re-layouts  6.65 us (4%)
  other arithmetic  5.89 us (4%)
  between operations  1.65 us (1%)
    ppermute x20, waiting for transfers between devices, hop(): return lax.ppermute(block, 'row', pairs)  67.8 us
    ppermute x20, starting transfers between devices, hop(): return lax.ppermute(block, 'row', pairs)  43.2 us
    pallas_call x3, Pallas kernels, run(): pl.pallas_call(kernel, grid=(1,), in_specs=in_specs, out_specs=[pl.BlockS...  25.7 us
    pallas_call x1, Pallas kernels, prepare(): pl.pallas_call(prepare_kernel, in_specs=[pl.BlockSpec(memory_space=pltpu....  6.65 us
    another operation x1, local copies, waits for them, and re-layouts, body(): turn = jnp.stack([jnp.cos(phase), jnp.sin(phase)])  3.69 us
  transfers between devices with their start and end apart: 20, of which 12 were waited for; matrix products, arithmetic and copies ran while one was open for 5% of the time, Pallas kernels for 10%

profile of v3, /device:TPU:38, one launch (start us, length us, event | category | flops | bytes accessed | tf_op | source)
XLA Modules:
  0.0 157.5 jit_solution(17406075483631904887)
XLA Ops:
  0.0 1.2 slice_bitcast_fusion.1
  1.2 23.1 %collective-permute-start.4 = (f32[2,128,768]{2,1,0:T(8,128)S(1)}, f32[2,128,768]{2,1,0:T(8,128)S(1)}, u32[]{:S(2)}, u32[]{:S(2)}) collective-permute-start(f32[2,128,768]{2,1,0:T(8,128)S(1)} %slice_bitcast_fusion.1), channel_id=1, source_target_pairs={{0,62},{1,63},{2,0},{3,1},{4,2},{5,3},{6,4},{7,5},{8,6},{9,7},{10,... | collective-permute-start | bytes 2359304 | tf_op jit(solution)/shard_map/ppermute | solution.py:15
  24.3 1.3 collective-permute-start.6
  25.8 17.4 %collective-permute-done.6 = s32[1]{0:T(128)} collective-permute-done((s32[1]{0:T(128)}, s32[1]{0:T(128)}, u32[]{:S(2)}, u32[]{:S(2)}) %collective-permute-start.6) | collective-permute-done | bytes 36 | tf_op jit(solution)/shard_map/ppermute | solution.py:15
  44.7 1.1 pad_maximum_fusion.1
  47.2 1.6 %copy-done.1 = f32[2,512,512]{2,1,0:T(8,128)S(1)} copy-done((f32[2,512,512]{2,1,0:T(8,128)S(1)}, f32[2,512,512]{2,1,0:T(8,128)}, u32[]{:S(2)}) %copy-start.1) | copy-done | bytes 2097176
  48.8 6.6 %prepare.1 = (bf16[2,512,512]{2,1,0:T(8,128)(2,1)S(1)}, bf16[2,512,512]{2,1,0:T(8,128)(2,1)S(1)}, bf16[1024,512]{1,0:T(8,128)(2,1)S(1)}, bf16[1024,512]{1,0:T(8,128)(2,1)S(1)}, f32[2,512,512]{2,1,0:T(8,128)S(1)}) custom-call(s32[3]{0:T(128)S(1)} %pad_add_fusion.place, f32[2,512,512]{2,1,0:T(8,128)S(1)} %copy-done.1), custom_call_target="tpu_custom_call" | custom-call | flops 16777216 | bytes 8388608 | tf_op jit(solution)/shard_map/prepare/pallas_call | solution.py:76
  56.1 1.7 %collective-permute-start.3 = (f32[2,128,768]{2,1,0:T(8,128)S(1)}, f32[2,128,768]{2,1,0:T(8,128)S(1)}, u32[]{:S(2)}, u32[]{:S(2)}) collective-permute-start(f32[2,128,768]{2,1,0:T(8,128)S(1)} %slice_bitcast_fusion), channel_id=1, source_target_pairs={{0,2},{1,3},{2,4},{3,5},{4,6},{5,7},{6,8},{7,9},{8,10},{9,11},{10,... | collective-permute-start | bytes 2359304 | tf_op jit(solution)/shard_map/ppermute | solution.py:15
  57.8 3.3 %collective-permute-start.8 = (f32[2,64,512]{2,1,0:T(8,128)S(1)}, f32[2,64,512]{2,1,0:T(8,128)S(1)}, u32[]{:S(2)}, u32[]{:S(2)}) collective-permute-start(f32[2,64,512]{2,1,0:T(8,128)S(1)} %pad_maximum_fusion.6), channel_id=1, source_target_pairs={{0,63},{2,1},{4,3},{6,5},{8,7},{10,9},{12,11},{14,13},{16,15},{18,... | collective-permute-start | bytes 786440 | tf_op jit(solution)/shard_map/ppermute | solution.py:15
  61.1 3.7 %cosine_bitcast_fusion = (f32[1,512,512]{2,1,0:T(8,128)S(1)}, f32[1,512,512]{2,1,0:T(8,128)S(1)}) fusion(f32[512,512]{1,0:T(8,128)S(1)} %copy-done.3), kind=kLoop, calls=%fused_computation.6 | loop fusion | bytes 3145728 | tf_op jit(solution)/shard_map/stack | solution.py:337
  65.0 2.9 %collective-permute-done.8.far = f32[2,64,512]{2,1,0:T(8,128)S(1)} collective-permute-done((f32[2,64,512]{2,1,0:T(8,128)S(1)}, f32[2,64,512]{2,1,0:T(8,128)S(1)}, u32[]{:S(2)}, u32[]{:S(2)}) %collective-permute-start.8) | collective-permute-done | bytes 262176 | tf_op jit(solution)/shard_map/ppermute | solution.py:15
  68.2 8.6 %shard_map.64.inner = f32[2,512,512]{2,1,0:T(8,128)S(1)} custom-call(s32[3]{0:T(128)S(1)} %pad_add_fusion.place, f32[2,2,128,768]{3,2,1,0:T(8,128)S(1)} %copy-done, f32[2,2,128,768]{3,2,1,0:T(8,128)} %collective-permute-done.partner, f32[2,128,768]{2,1,0:T(8,128)S(1)} %collective-permute-done.4.ahead, f32[2,128,768]{2,1,0:T(8,128)S(1)} %collective-permute-done.5.behind, ...), custom_call_target="tpu_custom_call" | custom-call | flops 4294967296 | bytes 16777216 | tf_op jit(solution)/shard_map/pallas_call | solution.py:252
  76.8 1.9 %collective-permute-done.2.bottom = f32[2,64,768]{2,1,0:T(8,128)S(1)} collective-permute-done((f32[2,64,768]{2,1,0:T(8,128)S(1)}, f32[2,64,768]{2,1,0:T(8,128)S(1)}, u32[]{:S(2)}, u32[]{:S(2)}) %collective-permute-start.2) | collective-permute-done | bytes 393248 | tf_op jit(solution)/shard_map/ppermute | solution.py:15
  78.9 1.2 collective-permute-start.9
  80.1 3.1 %collective-permute-start.10 = (f32[2,64,512]{2,1,0:T(8,128)S(1)}, f32[2,64,512]{2,1,0:T(8,128)S(1)}, u32[]{:S(2)}, u32[]{:S(2)}) collective-permute-start(f32[2,64,512]{2,1,0:T(8,128)S(1)} %pad_maximum_fusion.7), channel_id=1, source_target_pairs={{0,63},{2,1},{4,3},{6,5},{8,7},{10,9},{12,11},{14,13},{16,15},{18,... | collective-permute-start | bytes 786440 | tf_op jit(solution)/shard_map/ppermute | solution.py:15
  83.2 3.9 %collective-permute-done.10.far = f32[2,64,512]{2,1,0:T(8,128)S(1)} collective-permute-done((f32[2,64,512]{2,1,0:T(8,128)S(1)}, f32[2,64,512]{2,1,0:T(8,128)S(1)}, u32[]{:S(2)}, u32[]{:S(2)}) %collective-permute-start.10) | collective-permute-done | bytes 262176 | tf_op jit(solution)/shard_map/ppermute | solution.py:15
  87.0 9.5 %shard_map.65 = (f32[2,320,768]{2,1,0:T(8,128)S(1)}, f32[2,64,512]{2,1,0:T(8,128)S(1)}, f32[2,320,768]{2,1,0:T(8,128)S(1)}, bf16[1024,512]{1,0:T(8,128)(2,1)S(1)}) custom-call(s32[3]{0:T(128)S(1)} %pad_add_fusion.place, f32[2,2,128,768]{3,2,1,0:T(8,128)S(1)} %copy-done, f32[2,2,128,768]{3,2,1,0:T(8,128)} %collective-permute-done.partner, ...), custom_call_target="tpu_custom_call" | custom-call | flops 4294967296 | bytes 16777216 | tf_op jit(solution)/shard_map/pallas_call | solution.py:252
  96.6 0.9 collective-permute-start.11
  97.5 1.3 collective-permute-start.12
  98.8 0.6 iota_compare_fusion.1
  99.5 0.6 iota_compare_fusion
  100.1 6.3 %collective-permute-done.12 = f32[2,64,512]{2,1,0:T(8,128)S(1)} collective-permute-done((f32[2,64,512]{2,1,0:T(8,128)S(1)}, f32[2,64,512]{2,1,0:T(8,128)S(1)}, u32[]{:S(2)}, u32[]{:S(2)}) %collective-permute-start.12) | collective-permute-done | bytes 262176 | tf_op jit(solution)/shard_map/ppermute | solution.py:15
  106.7 7.6 %shard_map.66 = (f32[2,320,768]{2,1,0:T(8,128)S(1)}, f32[2,64,512]{2,1,0:T(8,128)S(1)}, f32[2,320,768]{2,1,0:T(8,128)S(1)}) custom-call(s32[3]{0:T(128)S(1)} %pad_add_fusion.place, bf16[1024,512]{1,0:T(8,128)(2,1)S(1)} %get-tuple-element.39.mid, f32[2,512,512]{2,1,0:T(8,128)S(1)} %get-tuple-element.26.light, f32[2,512,512]{2,1,0:T(8,128)S(1)} %pad_maximum_fusion.turn, ...), custom_call_target="tpu_custom_call" | custom-call | flops 4294967296 | bytes 16777216 | tf_op jit(solution)/shard_map/pallas_call | solution.py:252
  114.5 1.3 collective-permute-start.15
  115.9 1.6 %collective-permute-start.18 = (f32[2,128,768]{2,1,0:T(8,128)S(1)}, f32[2,128,768]{2,1,0:T(8,128)S(1)}, u32[]{:S(2)}, u32[]{:S(2)}) collective-permute-start(f32[2,128,768]{2,1,0:T(8,128)S(1)} %pad_maximum_fusion.5), channel_id=1, source_target_pairs={{0,62},{1,63},{2,0},{3,1},{4,2},{5,3},{6,4},{7,5},{8,6},{9,7},{10,... | collective-permute-start | bytes 2359304 | tf_op jit(solution)/shard_map/ppermute | solution.py:15
  118.7 2.4 %collective-permute-start.14 = (f32[2,128,768]{2,1,0:T(8,128)S(1)}, f32[2,128,768]{2,1,0:T(8,128)S(1)}, u32[]{:S(2)}, u32[]{:S(2)}) collective-permute-start(f32[2,128,768]{2,1,0:T(8,128)S(1)} %pad_maximum_fusion.4), channel_id=1, source_target_pairs={{0,62},{1,63},{2,0},{3,1},{4,2},{5,3},{6,4},{7,5},{8,6},{9,7},{10,... | collective-permute-start | bytes 2359304 | tf_op jit(solution)/shard_map/ppermute | solution.py:15
  121.0 3.6 %collective-permute-done.15 = f32[2,64,512]{2,1,0:T(8,128)S(1)} collective-permute-done((f32[2,64,512]{2,1,0:T(8,128)S(1)}, f32[2,64,512]{2,1,0:T(8,128)S(1)}, u32[]{:S(2)}, u32[]{:S(2)}) %collective-permute-start.15) | collective-permute-done | bytes 262176 | tf_op jit(solution)/shard_map/ppermute | solution.py:15
  125.0 11.4 %collective-permute-done.18 = f32[2,128,768]{2,1,0:T(8,128)S(1)} collective-permute-done((f32[2,128,768]{2,1,0:T(8,128)S(1)}, f32[2,128,768]{2,1,0:T(8,128)S(1)}, u32[]{:S(2)}, u32[]{:S(2)}) %collective-permute-start.18) | collective-permute-done | bytes 786464 | tf_op jit(solution)/shard_map/ppermute | solution.py:15
  136.4 2.7 %collective-permute-done.19 = f32[2,128,768]{2,1,0:T(8,128)S(1)} collective-permute-done((f32[2,128,768]{2,1,0:T(8,128)S(1)}, f32[2,128,768]{2,1,0:T(8,128)S(1)}, u32[]{:S(2)}, u32[]{:S(2)}) %collective-permute-start.19) | collective-permute-done | bytes 786464 | tf_op jit(solution)/shard_map/ppermute | solution.py:15
  139.3 8.2 %collective-permute-done.16 = f32[2,64,768]{2,1,0:T(8,128)S(1)} collective-permute-done((f32[2,64,768]{2,1,0:T(8,128)S(1)}, f32[2,64,768]{2,1,0:T(8,128)S(1)}, u32[]{:S(2)}, u32[]{:S(2)}) %collective-permute-start.16) | collective-permute-done | bytes 393248 | tf_op jit(solution)/shard_map/ppermute | solution.py:15
  147.5 8.4 %collective-permute-done.17 = f32[2,64,768]{2,1,0:T(8,128)S(1)} collective-permute-done((f32[2,64,768]{2,1,0:T(8,128)S(1)}, f32[2,64,768]{2,1,0:T(8,128)S(1)}, u32[]{:S(2)}, u32[]{:S(2)}) %collective-permute-start.17) | collective-permute-done | bytes 393248 | tf_op jit(solution)/shard_map/ppermute | solution.py:15
  156.2 1.4 fusion
  (51 shorter events, 5.4 us)
Async XLA Ops:
  1.2 42.7 %collective-permute-start.4 = (f32[2,128,768]{2,1,0:T(8,128)S(1)}, f32[2,128,768]{2,1,0:T(8,128)S(1)}, u32[]{:S(2)}, u32[]{:S(2)}) collective-permute-start(f32[2,128,768]{2,1,0:T(8,128)S(1)} %slice_bitcast_fusion.1), channel_id=1, source_target_pairs={{0,62},{1,63},{2,0},{3,1},{4,2},{5,3},{6,4},{7,5},{8,6},{9,7},{10,... | collective-permute-start | bytes 2359304 | tf_op jit(solution)/shard_map/ppermute | solution.py:15
  24.3 20.3 %collective-permute-start.5 = (f32[2,128,768]{2,1,0:T(8,128)S(1)}, f32[2,128,768]{2,1,0:T(8,128)S(1)}, u32[]{:S(2)}, u32[]{:S(2)}) collective-permute-start(f32[2,128,768]{2,1,0:T(8,128)S(1)} %slice_bitcast_fusion.1), channel_id=1, source_target_pairs={{0,2},{1,3},{2,4},{3,5},{4,6},{5,7},{6,8},{7,9},{8,10},{9,11},{10,... | collective-permute-start | bytes 2359304 | tf_op jit(solution)/shard_map/ppermute | solution.py:15
  24.3 18.9 %collective-permute-start.6 = (s32[1]{0:T(128)}, s32[1]{0:T(128)}, u32[]{:S(2)}, u32[]{:S(2)}) collective-permute-start(s32[1]{0:T(128)} %param.8), channel_id=1, source_target_pairs={{1,2},{3,4},{5,6},{7,8},{9,10},{11,12},{13,14},{15,16},{17,18},{19... | collective-permute-start | bytes 20 | tf_op jit(solution)/shard_map/ppermute | solution.py:15
  25.6 42.5 %collective-permute-start = (f32[2,2,128,768]{3,2,1,0:T(8,128)}, f32[2,2,128,768]{3,2,1,0:T(8,128)}, u32[]{:S(2)}, u32[]{:S(2)}) collective-permute-start(f32[2,2,128,768]{3,2,1,0:T(8,128)} %own.3), channel_id=1, source_target_pairs={{0,1},{1,0},{2,3},{3,2},{4,5},{5,4},{6,7},{7,6},{8,9},{9,8},{10,11... | collective-permute-start | bytes 4718600 | tf_op jit(solution)/shard_map/ppermute | solution.py:15
  44.7 10.7 %copy-start = (f32[2,2,128,768]{3,2,1,0:T(8,128)S(1)}, f32[2,2,128,768]{3,2,1,0:T(8,128)}, u32[]{:S(2)}) copy-start(f32[2,2,128,768]{3,2,1,0:T(8,128)} %own.3) | copy-start | bytes 4718596
  45.8 22.4 %collective-permute-start.7 = (f32[2,192,768]{2,1,0:T(8,128)}, f32[2,192,768]{2,1,0:T(8,128)}, u32[]{:S(2)}, u32[]{:S(2)}) collective-permute-start(f32[2,192,768]{2,1,0:T(8,128)} %pad_maximum_fusion.1), channel_id=1, source_target_pairs={{0,1},{1,0},{2,3},{3,2},{4,5},{5,4},{6,7},{7,6},{8,9},{9,8},{10,11... | collective-permute-start | bytes 3538952 | tf_op jit(solution)/shard_map/ppermute | solution.py:15
  47.2 1.6 %copy-start.1 = (f32[2,512,512]{2,1,0:T(8,128)S(1)}, f32[2,512,512]{2,1,0:T(8,128)}, u32[]{:S(2)}) copy-start(f32[2,512,512]{2,1,0:T(8,128)} %probe.1) | copy-start | bytes 6291460
  55.4 5.7 %copy-start.3 = (f32[512,512]{1,0:T(8,128)S(1)}, f32[512,512]{1,0:T(8,128)}, u32[]{:S(2)}) copy-start(f32[512,512]{1,0:T(8,128)} %param.11) | copy-start | bytes 3145732
  55.5 21.2 %collective-permute-start.1 = (f32[2,64,768]{2,1,0:T(8,128)S(1)}, f32[2,64,768]{2,1,0:T(8,128)S(1)}, u32[]{:S(2)}, u32[]{:S(2)}) collective-permute-start(f32[2,64,768]{2,1,0:T(8,128)S(1)} %get-tuple-element.53), channel_id=1, source_target_pairs={{0,62},{1,63},{2,0},{3,1},{4,2},{5,3},{6,4},{7,5},{8,6},{9,7},{10,... | collective-permute-start | bytes 1179656 | tf_op jit(solution)/shard_map/ppermute | solution.py:15
  56.1 22.6 %collective-permute-start.3 = (f32[2,128,768]{2,1,0:T(8,128)S(1)}, f32[2,128,768]{2,1,0:T(8,128)S(1)}, u32[]{:S(2)}, u32[]{:S(2)}) collective-permute-start(f32[2,128,768]{2,1,0:T(8,128)S(1)} %slice_bitcast_fusion), channel_id=1, source_target_pairs={{0,2},{1,3},{2,4},{3,5},{4,6},{5,7},{6,8},{7,9},{8,10},{9,11},{10,... | collective-permute-start | bytes 2359304 | tf_op jit(solution)/shard_map/ppermute | solution.py:15
  57.8 10.1 %collective-permute-start.8 = (f32[2,64,512]{2,1,0:T(8,128)S(1)}, f32[2,64,512]{2,1,0:T(8,128)S(1)}, u32[]{:S(2)}, u32[]{:S(2)}) collective-permute-start(f32[2,64,512]{2,1,0:T(8,128)S(1)} %pad_maximum_fusion.6), channel_id=1, source_target_pairs={{0,63},{2,1},{4,3},{6,5},{8,7},{10,9},{12,11},{14,13},{16,15},{18,... | collective-permute-start | bytes 786440 | tf_op jit(solution)/shard_map/ppermute | solution.py:15
  67.9 10.8 %collective-permute-start.2 = (f32[2,64,768]{2,1,0:T(8,128)S(1)}, f32[2,64,768]{2,1,0:T(8,128)S(1)}, u32[]{:S(2)}, u32[]{:S(2)}) collective-permute-start(f32[2,64,768]{2,1,0:T(8,128)S(1)} %get-tuple-element.52), channel_id=1, source_target_pairs={{0,62},{1,63},{2,0},{3,1},{4,2},{5,3},{6,4},{7,5},{8,6},{9,7},{10,... | collective-permute-start | bytes 1179656 | tf_op jit(solution)/shard_map/ppermute | solution.py:15
  78.8 8.3 %copy-start.2 = (f32[1,512,512]{2,1,0:T(8,128)S(1)}, f32[1,512,512]{2,1,0:T(8,128)}, u32[]{:S(2)}) copy-start(f32[1,512,512]{2,1,0:T(8,128)} %amplitude.1) | copy-start | bytes 3145732
  78.9 8.2 %collective-permute-start.9 = (f32[2,192,768]{2,1,0:T(8,128)S(1)}, f32[2,192,768]{2,1,0:T(8,128)S(1)}, u32[]{:S(2)}, u32[]{:S(2)}) collective-permute-start(f32[2,192,768]{2,1,0:T(8,128)S(1)} %pad_maximum_fusion.2), channel_id=1, source_target_pairs={{0,1},{1,0},{2,3},{3,2},{4,5},{5,4},{6,7},{7,6},{8,9},{9,8},{10,11... | collective-permute-start | bytes 3538952 | tf_op jit(solution)/shard_map/ppermute | solution.py:15
  80.1 6.9 %collective-permute-start.10 = (f32[2,64,512]{2,1,0:T(8,128)S(1)}, f32[2,64,512]{2,1,0:T(8,128)S(1)}, u32[]{:S(2)}, u32[]{:S(2)}) collective-permute-start(f32[2,64,512]{2,1,0:T(8,128)S(1)} %pad_maximum_fusion.7), channel_id=1, source_target_pairs={{0,63},{2,1},{4,3},{6,5},{8,7},{10,9},{12,11},{14,13},{16,15},{18,... | collective-permute-start | bytes 786440 | tf_op jit(solution)/shard_map/ppermute | solution.py:15
  96.6 9.9 %collective-permute-start.11 = (f32[2,320,768]{2,1,0:T(8,128)S(1)}, f32[2,320,768]{2,1,0:T(8,128)S(1)}, u32[]{:S(2)}, u32[]{:S(2)}) collective-permute-start(f32[2,320,768]{2,1,0:T(8,128)S(1)} %get-tuple-element.36), channel_id=1, source_target_pairs={{0,1},{1,0},{2,3},{3,2},{4,5},{5,4},{6,7},{7,6},{8,9},{9,8},{10,11... | collective-permute-start | bytes 5898248 | tf_op jit(solution)/shard_map/ppermute | solution.py:15
  97.5 8.9 %collective-permute-start.12 = (f32[2,64,512]{2,1,0:T(8,128)S(1)}, f32[2,64,512]{2,1,0:T(8,128)S(1)}, u32[]{:S(2)}, u32[]{:S(2)}) collective-permute-start(f32[2,64,512]{2,1,0:T(8,128)S(1)} %get-tuple-element.37), channel_id=1, source_target_pairs={{1,2},{3,4},{5,6},{7,8},{9,10},{11,12},{13,14},{15,16},{17,18},{19... | collective-permute-start | bytes 786440 | tf_op jit(solution)/shard_map/ppermute | solution.py:15
  114.4 4.1 %collective-permute-start.13 = (f32[2,320,768]{2,1,0:T(8,128)S(1)}, f32[2,320,768]{2,1,0:T(8,128)S(1)}, u32[]{:S(2)}, u32[]{:S(2)}) collective-permute-start(f32[2,320,768]{2,1,0:T(8,128)S(1)} %get-tuple-element.41), channel_id=1, source_target_pairs={{0,1},{1,0},{2,3},{3,2},{4,5},{5,4},{6,7},{7,6},{8,9},{9,8},{10,11... | collective-permute-start | bytes 5898248 | tf_op jit(solution)/shard_map/ppermute | solution.py:15
  114.5 10.1 %collective-permute-start.15 = (f32[2,64,512]{2,1,0:T(8,128)S(1)}, f32[2,64,512]{2,1,0:T(8,128)S(1)}, u32[]{:S(2)}, u32[]{:S(2)}) collective-permute-start(f32[2,64,512]{2,1,0:T(8,128)S(1)} %get-tuple-element.42), channel_id=1, source_target_pairs={{1,2},{3,4},{5,6},{7,8},{9,10},{11,12},{13,14},{15,16},{17,18},{19... | collective-permute-start | bytes 786440 | tf_op jit(solution)/shard_map/ppermute | solution.py:15
  115.9 20.5 %collective-permute-start.18 = (f32[2,128,768]{2,1,0:T(8,128)S(1)}, f32[2,128,768]{2,1,0:T(8,128)S(1)}, u32[]{:S(2)}, u32[]{:S(2)}) collective-permute-start(f32[2,128,768]{2,1,0:T(8,128)S(1)} %pad_maximum_fusion.5), channel_id=1, source_target_pairs={{0,62},{1,63},{2,0},{3,1},{4,2},{5,3},{6,4},{7,5},{8,6},{9,7},{10,... | collective-permute-start | bytes 2359304 | tf_op jit(solution)/shard_map/ppermute | solution.py:15
  117.5 21.6 %collective-permute-start.19 = (f32[2,128,768]{2,1,0:T(8,128)S(1)}, f32[2,128,768]{2,1,0:T(8,128)S(1)}, u32[]{:S(2)}, u32[]{:S(2)}) collective-permute-start(f32[2,128,768]{2,1,0:T(8,128)S(1)} %pad_maximum_fusion.3), channel_id=1, source_target_pairs={{0,2},{1,3},{2,4},{3,5},{4,6},{5,7},{6,8},{7,9},{8,10},{9,11},{10,... | collective-permute-start | bytes 2359304 | tf_op jit(solution)/shard_map/ppermute | solution.py:15
  118.7 37.3 %collective-permute-start.14 = (f32[2,128,768]{2,1,0:T(8,128)S(1)}, f32[2,128,768]{2,1,0:T(8,128)S(1)}, u32[]{:S(2)}, u32[]{:S(2)}) collective-permute-start(f32[2,128,768]{2,1,0:T(8,128)S(1)} %pad_maximum_fusion.4), channel_id=1, source_target_pairs={{0,62},{1,63},{2,0},{3,1},{4,2},{5,3},{6,4},{7,5},{8,6},{9,7},{10,... | collective-permute-start | bytes 2359304 | tf_op jit(solution)/shard_map/ppermute | solution.py:15
  124.8 22.8 %collective-permute-start.16 = (f32[2,64,768]{2,1,0:T(8,128)S(1)}, f32[2,64,768]{2,1,0:T(8,128)S(1)}, u32[]{:S(2)}, u32[]{:S(2)}) collective-permute-start(f32[2,64,768]{2,1,0:T(8,128)S(1)} %fusion.7), channel_id=1, source_target_pairs={{0,2},{1,3},{2,4},{3,5},{4,6},{5,7},{6,8},{7,9},{8,10},{9,11},{10,... | collective-permute-start | bytes 1179656 | tf_op jit(solution)/shard_map/ppermute | solution.py:15
  124.9 31.1 %collective-permute-start.17 = (f32[2,64,768]{2,1,0:T(8,128)S(1)}, f32[2,64,768]{2,1,0:T(8,128)S(1)}, u32[]{:S(2)}, u32[]{:S(2)}) collective-permute-start(f32[2,64,768]{2,1,0:T(8,128)S(1)} %get-tuple-element.45), channel_id=1, source_target_pairs={{0,2},{1,3},{2,4},{3,5},{4,6},{5,7},{6,8},{7,9},{8,10},{9,11},{10,... | collective-permute-start | bytes 1179656 | tf_op jit(solution)/shard_map/ppermute | solution.py:15

commit v4 on v3

--- a/solution.py
+++ b/solution.py
@@ -42,10 +42,11 @@
     return jnp.cos(angles), jnp.sin(angles)
 
 
-def prepare_kernel(place, probe, left, left_back, right, right_back, light, cos_base, sin_base):
+def prepare_kernel(place, far_col, probe, left, left_back, right, right_back, light, wraps, cos_base, sin_base):
     edge = probe.shape[1]
     fine = 32
     row, col = place[0], place[1]
+    wraps[...] = (lax.broadcasted_iota(jnp.int32, wraps.shape, 1) < far_col[0]).astype(jnp.float32)
     factor = 1.0 / math.sqrt(edge)
     fine_cos, fine_sin = wave_table(fine, 1, edge)
     coarse_cos, coarse_sin = wave_table(edge // fine, fine, edge)
@@ -69,20 +70,27 @@
     return [pl.BlockSpec(memory_space=VMEM)] * count
 
 
-def prepare(place, probe):
+def prepare(place, far_col, probe, half):
     edge = probe.shape[1]
     pair = jax.ShapeDtypeStruct((2, edge, edge), jnp.bfloat16)
     tall = jax.ShapeDtypeStruct((2 * edge, edge), jnp.bfloat16)
     return pl.pallas_call(
         prepare_kernel,
-        in_specs=[pl.BlockSpec(memory_space=pltpu.SMEM)] + whole(1),
-        out_specs=whole(5),
-        out_shape=[pair, pair, tall, tall, jax.ShapeDtypeStruct(probe.shape, jnp.float32)],
+        in_specs=[pl.BlockSpec(memory_space=pltpu.SMEM)] * 2 + whole(1),
+        out_specs=whole(6),
+        out_shape=[
+            pair,
+            pair,
+            tall,
+            tall,
+            jax.ShapeDtypeStruct(probe.shape, jnp.float32),
+            jax.ShapeDtypeStruct((half, edge), jnp.float32),
+        ],
         scratch_shapes=[VMEM((edge, edge), jnp.float32)] * 2,
         compiler_params=pltpu.CompilerParams(vmem_limit_bytes=16 << 20),
         cost_estimate=pl.CostEstimate(flops=16 << 20, bytes_accessed=8 << 20, transcendentals=0),
         name="prepare",
-    )(place, probe)
+    )(place, far_col, probe)
 
 
 def spectrum(field, left, right, back, emit):
@@ -279,28 +287,25 @@
     return lax.optimization_barrier((value,) + others)[0]
 
 
-def widened(x, start, cols):
-    edge = x.shape[2]
-    rest = cols - edge
-    column = lax.broadcasted_iota(jnp.int32, x.shape, 2)
-    kept = jnp.where(column >= start, x, 0.0)
-    wrapped = jnp.where(column < start, x, 0.0)[:, :, :rest]
+def widened(x, wraps, cols):
+    rest = cols - x.shape[2]
+    kept = jnp.where(wraps == 0.0, x, 0.0)
+    wrapped = jnp.where(wraps[:, :rest] == 0.0, 0.0, x[:, :, :rest])
     return jnp.concatenate([kept, wrapped], axis=2)
 
 
-def narrowed(x, start, edge):
+def narrowed(x, wraps, edge):
     rest = x.shape[2] - edge
-    column = lax.broadcasted_iota(jnp.int32, x.shape[:2] + (rest,), 2)
     return jnp.concatenate(
-        [jnp.where(column < start, x[:, :, edge:], x[:, :, :rest]), x[:, :, rest:edge]], axis=2
-    )
-
-
-def scattered(send, relay, keep, even, far_col, then):
+        [jnp.where(wraps[:, :rest] == 0.0, x[:, :, :rest], x[:, :, edge:]), x[:, :, rest:edge]], axis=2
+    )
+
+
+def scattered(send, relay, keep, even, wraps, then):
     half = relay.shape[1]
     block = lambda x, slot: x[:, slot * half : (slot + 1) * half]
+    got = swap(send)
     far = hop(relay, lambda i: i + 1 if i % 2 == 1 else None)
-    got = swap(send)
     to_bottom = block(keep, 3) + jnp.where(even, block(got, 3), 0.0)
     to_back = jnp.concatenate(
         [
@@ -310,15 +315,13 @@
         axis=1,
     )
     mine = keep[:, : 2 * half] + got[:, : 2 * half]
-    to_top = lambda far: block(keep, 2) + block(got, 2) + widened(far, far_col, keep.shape[2])
+    far = after(far, to_bottom, to_back)
+    to_top = block(keep, 2) + block(got, 2) + widened(far, wraps, keep.shape[2])
     if then is not None:
-        to_ahead, then = lax.optimization_barrier((jnp.concatenate([to_top(far), to_bottom], axis=1), then))
-        ahead = shift(to_ahead, 2)
-    else:
-        top = to_top(after(far, to_bottom, to_back))
-        ahead = [shift(to_bottom, 2)]
-        ahead = jnp.concatenate([shift(top, 2)] + ahead, axis=1)
-    return mine + shift(to_back, -2) + ahead, then
+        to_top, then = lax.optimization_barrier((to_top, then))
+    bottom = shift(to_bottom, 2)
+    top = shift(to_top, 2)
+    return mine + shift(to_back, -2) + jnp.concatenate([top, bottom], axis=1), then
 
 
 def body(object_field, row_offset, col_offset, amplitudes, probe, phase):
@@ -331,11 +334,13 @@
     lead = lax.optimization_barrier(object_field[0])
     rest_field = after(object_field, lead)
     ahead0 = shift(lead, -2)
-    far_col = hop(col_offset, lambda i: i + 1 if i % 2 == 1 else None)[0]
+    far_col = hop(col_offset, lambda i: i + 1 if i % 2 == 1 else None)
     behind0 = shift(lead, 2)
     partner = swap(rest_field)
     turn = jnp.stack([jnp.cos(phase), jnp.sin(phase)])
-    left, left_back, right, right_back, light = prepare(place, probe)
+    left, left_back, right, right_back, light, wraps = prepare(
+        after(place, turn), far_col, probe, half
+    )
 
     def crossing(ahead, behind, even):
         top, bottom = ahead
@@ -343,7 +348,7 @@
             [top, jnp.where(even, jnp.concatenate([bottom, bottom], axis=1), behind)], axis=1
         )
 
-    carried = lax.optimization_barrier(narrowed(ahead0[:, :half], far_col, edge))
+    carried = lax.optimization_barrier(narrowed(ahead0[:, :half], wraps, edge))
     far0 = hop(carried, lambda i: i - 1 if i % 2 == 0 else None)
     later_field = after(rest_field, light)
     top1 = shift(later_field[1, :, :half], -2)
@@ -368,7 +373,7 @@
     )
 
     top1_after, even_after = lax.optimization_barrier((top1, even, inner))[:2]
-    carried = narrowed(top1_after, far_col, edge)
+    carried = narrowed(top1_after, wraps, edge)
     far1 = hop(carried, lambda i: i - 1 if i % 2 == 0 else None)
     swapped1 = swap(crossing((top1_after, bottom1), behind1, even_after))
 
@@ -381,7 +386,7 @@
         piece_shapes(half, edge, cols) + [field],
         scratch,
     )
-    total2, mid = scattered(send, relay, keep, even, far_col, mid)
+    total2, mid = scattered(send, relay, keep, even, wraps, mid)
 
     arguments = (mid, light, turn) + waves
     send, relay, keep = run(
@@ -391,7 +396,7 @@
         piece_shapes(half, edge, cols),
         [scratch[0], scratch[2]],
     )
-    total1, _ = scattered(send, relay, keep, even, far_col, None)
+    total1, _ = scattered(send, relay, keep, even, wraps, None)
     return object_field - 0.5 * jnp.stack([total1, total2])
 
 

time: 160 us -> 154 us (0.963)
  waiting for transfers between devices: 67.8 us -> 62.1 us
  other arithmetic: 5.89 us -> 3.02 us
  starting transfers between devices: 43.2 us -> 45.9 us
    ppermute x20 -> x21, waiting for transfers between devices: 67.8 us -> 62.1 us  [hop(): return lax.ppermute(block, 'row', pairs)]
    ppermute x20 -> x21, starting transfers between devices: 43.2 us -> 45.9 us  [hop(): return lax.ppermute(block, 'row', pairs)]
    pallas_call x3, Pallas kernels: 25.7 us -> 23.8 us  [run(): pl.pallas_call(kernel, grid=(1,), in_specs=in_specs, out_specs=[pl.BlockS...]
  transfers between devices with their start and end apart: 20 -> 21, of which waited for: 12 -> 10; matrix products, arithmetic and copies ran while one was open for 5% -> 4% of each run, Pallas kernels for 10% -> 10%
where the time goes in v4:
time: 154 us; the launch traced here: 152 us
  waiting for transfers between devices  62.1 us (40%)
  starting transfers between devices  45.9 us (30%)
  Pallas kernels  30.9 us (20%)
  local copies, waits for them, and re-layouts  7.99 us (5%)
  other arithmetic  3.02 us (2%)
  between operations  1.68 us (1%)
    ppermute x21, waiting for transfers between devices, hop(): return lax.ppermute(block, 'row', pairs)  62.1 us
    ppermute x21, starting transfers between devices, hop(): return lax.ppermute(block, 'row', pairs)  45.9 us
    pallas_call x3, Pallas kernels, run(): pl.pallas_call(kernel, grid=(1,), in_specs=in_specs, out_specs=[pl.BlockS...  23.8 us
    pallas_call x1, Pallas kernels, prepare(): pl.pallas_call(prepare_kernel, in_specs=[pl.BlockSpec(memory_space=pltpu....  7.1 us
    another operation x1, local copies, waits for them, and re-layouts, body(): turn = jnp.stack([jnp.cos(phase), jnp.sin(phase)])  4.66 us
  transfers between devices with their start and end apart: 21, of which 10 were waited for; matrix products, arithmetic and copies ran while one was open for 4% of the time, Pallas kernels for 10%

profile of v4, /device:TPU:38, one launch (start us, length us, event | category | flops | bytes accessed | tf_op | source)
XLA Modules:
  0.0 151.6 jit_solution(556253227671397925)
XLA Ops:
  0.0 2.1 %slice_bitcast_fusion.1 = f32[2,128,768]{2,1,0:T(8,128)} fusion(f32[2,2,128,768]{3,2,1,0:T(8,128)} %own.3), kind=kLoop, calls=%fused_computation.20 | loop fusion | bytes 1572864 | tf_op jit(solution)/shard_map/squeeze | solution.py:334
  2.1 2.1 %collective-permute-start.6 = (f32[2,128,768]{2,1,0:T(8,128)}, f32[2,128,768]{2,1,0:T(8,128)S(1)}, u32[]{:S(2)}, u32[]{:S(2)}) collective-permute-start(f32[2,128,768]{2,1,0:T(8,128)} %slice_bitcast_fusion.1), channel_id=1, source_target_pairs={{0,2},{1,3},{2,4},{3,5},{4,6},{5,7},{6,8},{7,9},{8,10},{9,11},{10,... | collective-permute-start | bytes 2359304 | tf_op jit(solution)/shard_map/ppermute | solution.py:15
  4.2 20.9 %collective-permute-start.5 = (f32[2,128,768]{2,1,0:T(8,128)}, f32[2,128,768]{2,1,0:T(8,128)S(1)}, u32[]{:S(2)}, u32[]{:S(2)}) collective-permute-start(f32[2,128,768]{2,1,0:T(8,128)} %slice_bitcast_fusion.1), channel_id=1, source_target_pairs={{0,62},{1,63},{2,0},{3,1},{4,2},{5,3},{6,4},{7,5},{8,6},{9,7},{10,... | collective-permute-start | bytes 2359304 | tf_op jit(solution)/shard_map/ppermute | solution.py:15
  25.1 1.3 collective-permute-start.1
  28.0 4.7 %cosine_bitcast_fusion = (f32[1,512,512]{2,1,0:T(8,128)S(1)}, f32[1,512,512]{2,1,0:T(8,128)S(1)}) fusion(f32[512,512]{1,0:T(8,128)} %param.11), kind=kLoop, calls=%fused_computation.6 | loop fusion | bytes 3145728 | tf_op jit(solution)/shard_map/stack | solution.py:340
  32.7 0.2 pad_maximum_fusion.turn
  32.9 9.2 %collective-permute-done.1.far_col = s32[1]{0:T(128)} collective-permute-done((s32[1]{0:T(128)}, s32[1]{0:T(128)}, u32[]{:S(2)}, u32[]{:S(2)}) %collective-permute-start.1) | collective-permute-done | bytes 36 | tf_op jit(solution)/shard_map/ppermute | solution.py:15
  42.1 7.1 %prepare.1 = (bf16[2,512,512]{2,1,0:T(8,128)(2,1)S(1)}, bf16[2,512,512]{2,1,0:T(8,128)(2,1)S(1)}, bf16[1024,512]{1,0:T(8,128)(2,1)S(1)}, bf16[1024,512]{1,0:T(8,...) custom-call(s32[3]{0:T(128)S(1)} %pad_add_fusion.place, s32[1]{0:T(128)} %collective-permute-done.1.far_col, ...), custom_call_target="tpu_custom_call" | custom-call | flops 16777216 | bytes 8388608 | tf_op jit(solution)/shard_map/prepare/pallas_call | solution.py:77
  49.7 1.1 copy-done
  51.0 3.9 %collective-permute-start.8 = (f32[2,64,512]{2,1,0:T(8,128)S(1)}, f32[2,64,512]{2,1,0:T(8,128)S(1)}, u32[]{:S(2)}, u32[]{:S(2)}) collective-permute-start(f32[2,64,512]{2,1,0:T(8,128)S(1)} %pad_maximum_fusion.5), channel_id=1, source_target_pairs={{0,63},{2,1},{4,3},{6,5},{8,7},{10,9},{12,11},{14,13},{16,15},{18,... | collective-permute-start | bytes 786440 | tf_op jit(solution)/shard_map/ppermute | solution.py:15
  54.9 0.9 collective-permute-start.3
  55.9 5.7 %collective-permute-done.8.far = f32[2,64,512]{2,1,0:T(8,128)S(1)} collective-permute-done((f32[2,64,512]{2,1,0:T(8,128)S(1)}, f32[2,64,512]{2,1,0:T(8,128)S(1)}, u32[]{:S(2)}, u32[]{:S(2)}) %collective-permute-start.8) | collective-permute-done | bytes 262176 | tf_op jit(solution)/shard_map/ppermute | solution.py:15
  61.5 0.6 collective-permute-start.2
  62.2 7.5 %shard_map.64.inner = f32[2,512,512]{2,1,0:T(8,128)S(1)} custom-call(s32[3]{0:T(128)S(1)} %pad_add_fusion.place, f32[2,2,128,768]{3,2,1,0:T(8,128)S(1)} %copy-done, f32[2,2,128,768]{3,2,1,0:T(8,128)S(1)} %collective-permute-done.partner, f32[2,128,768]{2,1,0:T(8,128)S(1)} %collective-permute-done.5.ahead, f32[2,128,768]{2,1,0:T(8,128)S(1)} %collective-permute-done.6.behind, ...), custom_call_target="tpu_custom_call" | custom-call | flops 4294967296 | bytes 16777216 | tf_op jit(solution)/shard_map/pallas_call | solution.py:260
  69.7 5.1 %collective-permute-done.2.top = f32[2,64,768]{2,1,0:T(8,128)S(1)} collective-permute-done((f32[2,64,768]{2,1,0:T(8,128)S(1)}, f32[2,64,768]{2,1,0:T(8,128)S(1)}, u32[]{:S(2)}, u32[]{:S(2)}) %collective-permute-start.2) | collective-permute-done | bytes 393248 | tf_op jit(solution)/shard_map/ppermute | solution.py:15
  75.1 5.7 %collective-permute-start.10 = (f32[2,64,512]{2,1,0:T(8,128)S(1)}, f32[2,64,512]{2,1,0:T(8,128)S(1)}, u32[]{:S(2)}, u32[]{:S(2)}) collective-permute-start(f32[2,64,512]{2,1,0:T(8,128)S(1)} %pad_maximum_fusion.6), channel_id=1, source_target_pairs={{0,63},{2,1},{4,3},{6,5},{8,7},{10,9},{12,11},{14,13},{16,15},{18,... | collective-permute-start | bytes 786440 | tf_op jit(solution)/shard_map/ppermute | solution.py:15
  80.9 3.9 %collective-permute-done.10.far = f32[2,64,512]{2,1,0:T(8,128)S(1)} collective-permute-done((f32[2,64,512]{2,1,0:T(8,128)S(1)}, f32[2,64,512]{2,1,0:T(8,128)S(1)}, u32[]{:S(2)}, u32[]{:S(2)}) %collective-permute-start.10) | collective-permute-done | bytes 262176 | tf_op jit(solution)/shard_map/ppermute | solution.py:15
  84.7 8.8 %shard_map.65 = (f32[2,320,768]{2,1,0:T(8,128)S(1)}, f32[2,64,512]{2,1,0:T(8,128)S(1)}, f32[2,320,768]{2,1,0:T(8,128)S(1)}, bf16[1024,512]{1,0:T(8,128)(2,1)S(1)}) custom-call(s32[3]{0:T(128)S(1)} %pad_add_fusion.place, f32[2,2,128,768]{3,2,1,0:T(8,128)S(1)} %copy-done, f32[2,2,128,768]{3,2,1,0:T(8,128)S(1)} %collective-permute-done.partner, ...), custom_call_target="tpu_custom_call" | custom-call | flops 4294967296 | bytes 16777216 | tf_op jit(solution)/shard_map/pallas_call | solution.py:260
  93.7 1.3 collective-permute-start.12
  95.0 2.6 %collective-permute-done.11 = f32[2,320,768]{2,1,0:T(8,128)S(1)} collective-permute-done((f32[2,320,768]{2,1,0:T(8,128)S(1)}, f32[2,320,768]{2,1,0:T(8,128)S(1)}, u32[]{:S(2)}, u32[]{:S(2)}) %collective-permute-start.11) | collective-permute-done | bytes 1966112 | tf_op jit(solution)/shard_map/ppermute | solution.py:15
  97.8 4.8 %collective-permute-done.12 = f32[2,64,512]{2,1,0:T(8,128)S(1)} collective-permute-done((f32[2,64,512]{2,1,0:T(8,128)S(1)}, f32[2,64,512]{2,1,0:T(8,128)S(1)}, u32[]{:S(2)}, u32[]{:S(2)}) %collective-permute-start.12) | collective-permute-done | bytes 262176 | tf_op jit(solution)/shard_map/ppermute | solution.py:15
  102.7 7.6 %shard_map.66 = (f32[2,320,768]{2,1,0:T(8,128)S(1)}, f32[2,64,512]{2,1,0:T(8,128)S(1)}, f32[2,320,768]{2,1,0:T(8,128)S(1)}) custom-call(s32[3]{0:T(128)S(1)} %pad_add_fusion.place, bf16[1024,512]{1,0:T(8,128)(2,1)S(1)} %get-tuple-element.45.mid, f32[2,512,512]{2,1,0:T(8,128)S(1)} %get-tuple-element.30.light, f32[2,512,512]{2,1,0:T(8,128)S(1)} %pad_maximum_fusion.turn, ...), custom_call_target="tpu_custom_call" | custom-call | flops 4294967296 | bytes 16777216 | tf_op jit(solution)/shard_map/pallas_call | solution.py:260
  110.6 3.2 %collective-permute-start.18 = (f32[2,128,768]{2,1,0:T(8,128)S(1)}, f32[2,128,768]{2,1,0:T(8,128)S(1)}, u32[]{:S(2)}, u32[]{:S(2)}) collective-permute-start(f32[2,128,768]{2,1,0:T(8,128)S(1)} %pad_maximum_fusion.3), channel_id=1, source_target_pairs={{0,62},{1,63},{2,0},{3,1},{4,2},{5,3},{6,4},{7,5},{8,6},{9,7},{10,... | collective-permute-start | bytes 2359304 | tf_op jit(solution)/shard_map/ppermute | solution.py:15
  113.8 1.3 collective-permute-start.15
  115.5 3.3 %collective-permute-start.14 = (f32[2,128,768]{2,1,0:T(8,128)S(1)}, f32[2,128,768]{2,1,0:T(8,128)S(1)}, u32[]{:S(2)}, u32[]{:S(2)}) collective-permute-start(f32[2,128,768]{2,1,0:T(8,128)S(1)} %pad_maximum_fusion.4), channel_id=1, source_target_pairs={{0,62},{1,63},{2,0},{3,1},{4,2},{5,3},{6,4},{7,5},{8,6},{9,7},{10,... | collective-permute-start | bytes 2359304 | tf_op jit(solution)/shard_map/ppermute | solution.py:15
  118.8 9.4 %collective-permute-done.15 = f32[2,64,512]{2,1,0:T(8,128)S(1)} collective-permute-done((f32[2,64,512]{2,1,0:T(8,128)S(1)}, f32[2,64,512]{2,1,0:T(8,128)S(1)}, u32[]{:S(2)}, u32[]{:S(2)}) %collective-permute-start.15) | collective-permute-done | bytes 262176 | tf_op jit(solution)/shard_map/ppermute | solution.py:15
  128.5 3.7 %collective-permute-done.19 = f32[2,64,768]{2,1,0:T(8,128)S(1)} collective-permute-done((f32[2,64,768]{2,1,0:T(8,128)S(1)}, f32[2,64,768]{2,1,0:T(8,128)S(1)}, u32[]{:S(2)}, u32[]{:S(2)}) %collective-permute-start.19) | collective-permute-done | bytes 393248 | tf_op jit(solution)/shard_map/ppermute | solution.py:15
  132.2 0.2 fusion.3
  132.4 9.2 %collective-permute-done.16 = f32[2,64,768]{2,1,0:T(8,128)S(1)} collective-permute-done((f32[2,64,768]{2,1,0:T(8,128)S(1)}, f32[2,64,768]{2,1,0:T(8,128)S(1)}, u32[]{:S(2)}, u32[]{:S(2)}) %collective-permute-start.16) | collective-permute-done | bytes 393248 | tf_op jit(solution)/shard_map/ppermute | solution.py:15
  141.6 8.4 %collective-permute-done.17 = f32[2,64,768]{2,1,0:T(8,128)S(1)} collective-permute-done((f32[2,64,768]{2,1,0:T(8,128)S(1)}, f32[2,64,768]{2,1,0:T(8,128)S(1)}, u32[]{:S(2)}, u32[]{:S(2)}) %collective-permute-start.17) | collective-permute-done | bytes 393248 | tf_op jit(solution)/shard_map/ppermute | solution.py:15
  150.1 0.2 fusion.6
  150.3 1.3 fusion
  (50 shorter events, 2.6 us)
Async XLA Ops:
  2.1 47.3 %collective-permute-start.6 = (f32[2,128,768]{2,1,0:T(8,128)}, f32[2,128,768]{2,1,0:T(8,128)S(1)}, u32[]{:S(2)}, u32[]{:S(2)}) collective-permute-start(f32[2,128,768]{2,1,0:T(8,128)} %slice_bitcast_fusion.1), channel_id=1, source_target_pairs={{0,2},{1,3},{2,4},{3,5},{4,6},{5,7},{6,8},{7,9},{8,10},{9,11},{10,... | collective-permute-start | bytes 2359304 | tf_op jit(solution)/shard_map/ppermute | solution.py:15
  4.2 45.0 %collective-permute-start.5 = (f32[2,128,768]{2,1,0:T(8,128)}, f32[2,128,768]{2,1,0:T(8,128)S(1)}, u32[]{:S(2)}, u32[]{:S(2)}) collective-permute-start(f32[2,128,768]{2,1,0:T(8,128)} %slice_bitcast_fusion.1), channel_id=1, source_target_pairs={{0,62},{1,63},{2,0},{3,1},{4,2},{5,3},{6,4},{7,5},{8,6},{9,7},{10,... | collective-permute-start | bytes 2359304 | tf_op jit(solution)/shard_map/ppermute | solution.py:15
  25.1 17.0 %collective-permute-start.1 = (s32[1]{0:T(128)}, s32[1]{0:T(128)}, u32[]{:S(2)}, u32[]{:S(2)}) collective-permute-start(s32[1]{0:T(128)} %param.8), channel_id=1, source_target_pairs={{1,2},{3,4},{5,6},{7,8},{9,10},{11,12},{13,14},{15,16},{17,18},{19... | collective-permute-start | bytes 20 | tf_op jit(solution)/shard_map/ppermute | solution.py:15
  26.4 35.8 %collective-permute-start = (f32[2,2,128,768]{3,2,1,0:T(8,128)}, f32[2,2,128,768]{3,2,1,0:T(8,128)S(1)}, u32[]{:S(2)}, u32[]{:S(2)}) collective-permute-start(f32[2,2,128,768]{3,2,1,0:T(8,128)} %own.3), channel_id=1, source_target_pairs={{0,1},{1,0},{2,3},{3,2},{4,5},{5,4},{6,7},{7,6},{8,9},{9,8},{10,11... | collective-permute-start | bytes 4718600 | tf_op jit(solution)/shard_map/ppermute | solution.py:15
  32.6 9.4 %copy-start.1 = (f32[2,512,512]{2,1,0:T(8,128)S(1)}, f32[2,512,512]{2,1,0:T(8,128)}, u32[]{:S(2)}) copy-start(f32[2,512,512]{2,1,0:T(8,128)} %probe.1) | copy-start | bytes 6291460
  49.4 1.4 copy-start
  49.5 12.6 %collective-permute-start.7 = (f32[2,192,768]{2,1,0:T(8,128)S(1)}, f32[2,192,768]{2,1,0:T(8,128)S(1)}, u32[]{:S(2)}, u32[]{:S(2)}) collective-permute-start(f32[2,192,768]{2,1,0:T(8,128)S(1)} %pad_maximum_fusion.1), channel_id=1, source_target_pairs={{0,1},{1,0},{2,3},{3,2},{4,5},{5,4},{6,7},{7,6},{8,9},{9,8},{10,11... | collective-permute-start | bytes 3538952 | tf_op jit(solution)/shard_map/ppermute | solution.py:15
  50.8 23.9 %collective-permute-start.4 = (f32[2,128,768]{2,1,0:T(8,128)S(1)}, f32[2,128,768]{2,1,0:T(8,128)S(1)}, u32[]{:S(2)}, u32[]{:S(2)}) collective-permute-start(f32[2,128,768]{2,1,0:T(8,128)S(1)} %slice_bitcast_fusion), channel_id=1, source_target_pairs={{0,2},{1,3},{2,4},{3,5},{4,6},{5,7},{6,8},{7,9},{8,10},{9,11},{10,... | collective-permute-start | bytes 2359304 | tf_op jit(solution)/shard_map/ppermute | solution.py:15
  51.0 10.5 %collective-permute-start.8 = (f32[2,64,512]{2,1,0:T(8,128)S(1)}, f32[2,64,512]{2,1,0:T(8,128)S(1)}, u32[]{:S(2)}, u32[]{:S(2)}) collective-permute-start(f32[2,64,512]{2,1,0:T(8,128)S(1)} %pad_maximum_fusion.5), channel_id=1, source_target_pairs={{0,63},{2,1},{4,3},{6,5},{8,7},{10,9},{12,11},{14,13},{16,15},{18,... | collective-permute-start | bytes 786440 | tf_op jit(solution)/shard_map/ppermute | solution.py:15
  54.9 19.8 %collective-permute-start.3 = (f32[2,64,768]{2,1,0:T(8,128)S(1)}, f32[2,64,768]{2,1,0:T(8,128)S(1)}, u32[]{:S(2)}, u32[]{:S(2)}) collective-permute-start(f32[2,64,768]{2,1,0:T(8,128)S(1)} %get-tuple-element.57), channel_id=1, source_target_pairs={{0,62},{1,63},{2,0},{3,1},{4,2},{5,3},{6,4},{7,5},{8,6},{9,7},{10,... | collective-permute-start | bytes 1179656 | tf_op jit(solution)/shard_map/ppermute | solution.py:15
  61.5 13.2 %collective-permute-start.2 = (f32[2,64,768]{2,1,0:T(8,128)S(1)}, f32[2,64,768]{2,1,0:T(8,128)S(1)}, u32[]{:S(2)}, u32[]{:S(2)}) collective-permute-start(f32[2,64,768]{2,1,0:T(8,128)S(1)} %get-tuple-element.58), channel_id=1, source_target_pairs={{0,62},{1,63},{2,0},{3,1},{4,2},{5,3},{6,4},{7,5},{8,6},{9,7},{10,... | collective-permute-start | bytes 1179656 | tf_op jit(solution)/shard_map/ppermute | solution.py:15
  74.8 9.9 %copy-start.2 = (f32[1,512,512]{2,1,0:T(8,128)S(1)}, f32[1,512,512]{2,1,0:T(8,128)}, u32[]{:S(2)}) copy-start(f32[1,512,512]{2,1,0:T(8,128)} %amplitude.1) | copy-start | bytes 3145732
  74.9 9.8 %collective-permute-start.9 = (f32[2,192,768]{2,1,0:T(8,128)S(1)}, f32[2,192,768]{2,1,0:T(8,128)S(1)}, u32[]{:S(2)}, u32[]{:S(2)}) collective-permute-start(f32[2,192,768]{2,1,0:T(8,128)S(1)} %pad_maximum_fusion.2), channel_id=1, source_target_pairs={{0,1},{1,0},{2,3},{3,2},{4,5},{5,4},{6,7},{7,6},{8,9},{9,8},{10,11... | collective-permute-start | bytes 3538952 | tf_op jit(solution)/shard_map/ppermute | solution.py:15
  75.1 9.6 %collective-permute-start.10 = (f32[2,64,512]{2,1,0:T(8,128)S(1)}, f32[2,64,512]{2,1,0:T(8,128)S(1)}, u32[]{:S(2)}, u32[]{:S(2)}) collective-permute-start(f32[2,64,512]{2,1,0:T(8,128)S(1)} %pad_maximum_fusion.6), channel_id=1, source_target_pairs={{0,63},{2,1},{4,3},{6,5},{8,7},{10,9},{12,11},{14,13},{16,15},{18,... | collective-permute-start | bytes 786440 | tf_op jit(solution)/shard_map/ppermute | solution.py:15
  93.5 4.1 %collective-permute-start.11 = (f32[2,320,768]{2,1,0:T(8,128)S(1)}, f32[2,320,768]{2,1,0:T(8,128)S(1)}, u32[]{:S(2)}, u32[]{:S(2)}) collective-permute-start(f32[2,320,768]{2,1,0:T(8,128)S(1)} %get-tuple-element.41), channel_id=1, source_target_pairs={{0,1},{1,0},{2,3},{3,2},{4,5},{5,4},{6,7},{7,6},{8,9},{9,8},{10,11... | collective-permute-start | bytes 5898248 | tf_op jit(solution)/shard_map/ppermute | solution.py:15
  93.7 8.9 %collective-permute-start.12 = (f32[2,64,512]{2,1,0:T(8,128)S(1)}, f32[2,64,512]{2,1,0:T(8,128)S(1)}, u32[]{:S(2)}, u32[]{:S(2)}) collective-permute-start(f32[2,64,512]{2,1,0:T(8,128)S(1)} %get-tuple-element.42), channel_id=1, source_target_pairs={{1,2},{3,4},{5,6},{7,8},{9,10},{11,12},{13,14},{15,16},{17,18},{19... | collective-permute-start | bytes 786440 | tf_op jit(solution)/shard_map/ppermute | solution.py:15
  110.3 4.9 %collective-permute-start.13 = (f32[2,320,768]{2,1,0:T(8,128)S(1)}, f32[2,320,768]{2,1,0:T(8,128)S(1)}, u32[]{:S(2)}, u32[]{:S(2)}) collective-permute-start(f32[2,320,768]{2,1,0:T(8,128)S(1)} %get-tuple-element.47), channel_id=1, source_target_pairs={{0,1},{1,0},{2,3},{3,2},{4,5},{5,4},{6,7},{7,6},{8,9},{9,8},{10,11... | collective-permute-start | bytes 5898248 | tf_op jit(solution)/shard_map/ppermute | solution.py:15
  110.5 21.7 %collective-permute-start.20 = (f32[2,64,768]{2,1,0:T(8,128)S(1)}, f32[2,64,768]{2,1,0:T(8,128)S(1)}, u32[]{:S(2)}, u32[]{:S(2)}) collective-permute-start(f32[2,64,768]{2,1,0:T(8,128)S(1)} %get-tuple-element.53), channel_id=1, source_target_pairs={{0,2},{1,3},{2,4},{3,5},{4,6},{5,7},{6,8},{7,9},{8,10},{9,11},{10,... | collective-permute-start | bytes 1179656 | tf_op jit(solution)/shard_map/ppermute | solution.py:15
  110.6 21.6 %collective-permute-start.18 = (f32[2,128,768]{2,1,0:T(8,128)S(1)}, f32[2,128,768]{2,1,0:T(8,128)S(1)}, u32[]{:S(2)}, u32[]{:S(2)}) collective-permute-start(f32[2,128,768]{2,1,0:T(8,128)S(1)} %pad_maximum_fusion.3), channel_id=1, source_target_pairs={{0,62},{1,63},{2,0},{3,1},{4,2},{5,3},{6,4},{7,5},{8,6},{9,7},{10,... | collective-permute-start | bytes 2359304 | tf_op jit(solution)/shard_map/ppermute | solution.py:15
  113.8 14.4 %collective-permute-start.15 = (f32[2,64,512]{2,1,0:T(8,128)S(1)}, f32[2,64,512]{2,1,0:T(8,128)S(1)}, u32[]{:S(2)}, u32[]{:S(2)}) collective-permute-start(f32[2,64,512]{2,1,0:T(8,128)S(1)} %get-tuple-element.48), channel_id=1, source_target_pairs={{1,2},{3,4},{5,6},{7,8},{9,10},{11,12},{13,14},{15,16},{17,18},{19... | collective-permute-start | bytes 786440 | tf_op jit(solution)/shard_map/ppermute | solution.py:15
  115.1 17.1 %collective-permute-start.19 = (f32[2,64,768]{2,1,0:T(8,128)S(1)}, f32[2,64,768]{2,1,0:T(8,128)S(1)}, u32[]{:S(2)}, u32[]{:S(2)}) collective-permute-start(f32[2,64,768]{2,1,0:T(8,128)S(1)} %fusion.8), channel_id=1, source_target_pairs={{0,2},{1,3},{2,4},{3,5},{4,6},{5,7},{6,8},{7,9},{8,10},{9,11},{10,... | collective-permute-start | bytes 1179656 | tf_op jit(solution)/shard_map/ppermute | solution.py:15
  115.5 34.6 %collective-permute-start.14 = (f32[2,128,768]{2,1,0:T(8,128)S(1)}, f32[2,128,768]{2,1,0:T(8,128)S(1)}, u32[]{:S(2)}, u32[]{:S(2)}) collective-permute-start(f32[2,128,768]{2,1,0:T(8,128)S(1)} %pad_maximum_fusion.4), channel_id=1, source_target_pairs={{0,62},{1,63},{2,0},{3,1},{4,2},{5,3},{6,4},{7,5},{8,6},{9,7},{10,... | collective-permute-start | bytes 2359304 | tf_op jit(solution)/shard_map/ppermute | solution.py:15
  128.3 13.3 %collective-permute-start.16 = (f32[2,64,768]{2,1,0:T(8,128)S(1)}, f32[2,64,768]{2,1,0:T(8,128)S(1)}, u32[]{:S(2)}, u32[]{:S(2)}) collective-permute-start(f32[2,64,768]{2,1,0:T(8,128)S(1)} %fusion.7), channel_id=1, source_target_pairs={{0,2},{1,3},{2,4},{3,5},{4,6},{5,7},{6,8},{7,9},{8,10},{9,11},{10,... | collective-permute-start | bytes 1179656 | tf_op jit(solution)/shard_map/ppermute | solution.py:15
  132.2 17.9 %collective-permute-start.17 = (f32[2,64,768]{2,1,0:T(8,128)S(1)}, f32[2,64,768]{2,1,0:T(8,128)S(1)}, u32[]{:S(2)}, u32[]{:S(2)}) collective-permute-start(f32[2,64,768]{2,1,0:T(8,128)S(1)} %get-tuple-element.51), channel_id=1, source_target_pairs={{0,2},{1,3},{2,4},{3,5},{4,6},{5,7},{6,8},{7,9},{8,10},{9,11},{10,... | collective-permute-start | bytes 1179656 | tf_op jit(solution)/shard_map/ppermute | solution.py:15
